TPU v7x, 32 devices: a whole 2x2x4 slice. The times are simulated.
32 devices in a mesh: batch: 2 (over x), sy: 4 (over z), sx: 4 (over y, core).
Axes of the slice: x: 2, y: 2, z: 4, core: 2. Of those that a mesh axis runs over, the one named last changes fastest.
Arguments:
- forcing: float32 [256, 128, 256], P(('batch', 'sx'), 'sy'), parts along dimension 0
- kappa: float32 [256, 128], P(('batch', 'sx'), 'sy'), parts along dimension 0
- local_inv: float32 [32, 1600, 1600], P(('batch', 'sx', 'sy')), parts along dimension 0
- coarse_basis: float32 [32, 1024, 8], P(('batch', 'sx', 'sy')), parts along dimension 0
- coarse_counts: int32 [32], P(('batch', 'sx', 'sy')), parts along dimension 0
- coarse_inv: float32 [128, 64], P('batch'), parts along dimension 0
Outputs:
- output 1: float32 [256, 128, 256], P(('batch', 'sx'), 'sy'), parts along dimension 0
- output 2: float32 [16, 256], P('batch'), parts along dimension 0
There are 2 independent parts. A program takes and returns all parts, laid end to end along the dimension named above; each array names one.
All inputs are finite; a program needn't handle non-finite values.
Results may differ from a plain program's by a relative error of at most 0.001.
Values are sent between devices in bfloat16 or wider.
A program may use at most 1 GiB of HBM per device.

v0:
```python
import math
import jax
import jax.numpy as jnp
from jax import lax
from jax.sharding import PartitionSpec as P

ITERS = 8


def harmonic(first, second):
    return 2.0 * first * second / (first + second)


def solution(mesh):
    n_row = mesh.shape['sx']
    n_col = mesh.shape['sy']
    to_below = [(index, index + 1) for index in range(n_row - 1)]
    to_above = [(index + 1, index) for index in range(n_row - 1)]
    to_right = [(index, index + 1) for index in range(n_col - 1)]
    to_left = [(index + 1, index) for index in range(n_col - 1)]
    grid_axes = ('sx', 'sy')
    highest = lax.Precision.HIGHEST

    def matmul(first, second):
        return jnp.dot(first, second, precision=highest, preferred_element_type=jnp.float32)

    def body(forcing, kappa, local_inv, coarse_basis, coarse_counts, coarse_inv):
        row_id = lax.axis_index('sx')
        col_id = lax.axis_index('sy')
        size = forcing.shape[0]
        n_rhs = forcing.shape[2]
        edge = math.isqrt(local_inv.shape[1])
        over = (edge - size) // 2
        kmax = coarse_basis.shape[2]
        ktot = coarse_inv.shape[0]
        inverse = local_inv[0]
        basis = coarse_basis[0]

        above = lax.ppermute(kappa[-1:], 'sx', to_below)
        below = lax.ppermute(kappa[:1], 'sx', to_above)
        leftside = lax.ppermute(kappa[:, -1:], 'sy', to_right)
        rightside = lax.ppermute(kappa[:, :1], 'sy', to_left)
        above = jnp.where(row_id == 0, kappa[:1], above)
        below = jnp.where(row_id == n_row - 1, kappa[-1:], below)
        leftside = jnp.where(col_id == 0, kappa[:, :1], leftside)
        rightside = jnp.where(col_id == n_col - 1, kappa[:, -1:], rightside)
        w_north = harmonic(kappa, jnp.concatenate([above, kappa[:-1]], axis=0))[:, :, None]
        w_south = harmonic(kappa, jnp.concatenate([kappa[1:], below], axis=0))[:, :, None]
        w_west = harmonic(kappa, jnp.concatenate([leftside, kappa[:, :-1]], axis=1))[:, :, None]
        w_east = harmonic(kappa, jnp.concatenate([kappa[:, 1:], rightside], axis=1))[:, :, None]
        diagonal = w_north + w_south + w_west + w_east

        counts_all = lax.all_gather(coarse_counts, grid_axes, tiled=True)
        n_sub = counts_all.shape[0]
        starts = jnp.cumsum(counts_all) - counts_all
        slot = jnp.arange(n_sub * kmax)
        owner = slot // kmax
        column = slot % kmax
        target = jnp.where(column < counts_all[owner], starts[owner] + column, -1)
        pack_mat = (jnp.arange(ktot)[:, None] == target[None, :]).astype(jnp.float32)
        self_index = row_id * n_col + col_id
        own_slots = jnp.arange(kmax)
        own_target = jnp.where(own_slots < counts_all[self_index], starts[self_index] + own_slots, -1)
        pick_mat = (own_target[:, None] == jnp.arange(ktot)[None, :]).astype(jnp.float32)
        own_map = matmul(matmul(pick_mat, coarse_inv), pack_mat)

        def apply_local(field):
            from_top = lax.ppermute(field[-1:], 'sx', to_below)
            from_bottom = lax.ppermute(field[:1], 'sx', to_above)
            from_left = lax.ppermute(field[:, -1:], 'sy', to_right)
            from_right = lax.ppermute(field[:, :1], 'sy', to_left)
            north = jnp.concatenate([from_top, field[:-1]], axis=0)
            south = jnp.concatenate([field[1:], from_bottom], axis=0)
            west = jnp.concatenate([from_left, field[:, :-1]], axis=1)
            east = jnp.concatenate([field[:, 1:], from_right], axis=1)
            return diagonal * field - w_north * north - w_south * south - w_west * west - w_east * east

        def schwarz(resid):
            from_top = lax.ppermute(resid[size - over:], 'sx', to_below)
            from_bottom = lax.ppermute(resid[:over], 'sx', to_above)
            tall = jnp.concatenate([from_top, resid, from_bottom], axis=0)
            from_left = lax.ppermute(tall[:, size - over:], 'sy', to_right)
            from_right = lax.ppermute(tall[:, :over], 'sy', to_left)
            extended = jnp.concatenate([from_left, tall, from_right], axis=1)
            local = matmul(inverse, extended.reshape(edge * edge, n_rhs)).reshape(edge, edge, n_rhs)
            back_left = lax.ppermute(local[:, :over], 'sy', to_left)
            back_right = lax.ppermute(local[:, size + over:], 'sy', to_right)
            wide = (local[:, over:over + size] + jnp.pad(back_left, ((0, 0), (size - over, 0), (0, 0))) + jnp.pad(back_right, ((0, 0), (0, size - over), (0, 0))))
            back_up = lax.ppermute(wide[:over], 'sx', to_above)
            back_down = lax.ppermute(wide[size + over:], 'sx', to_below)
            level_one = (wide[over:over + size] + jnp.pad(back_up, ((size - over, 0), (0, 0), (0, 0))) + jnp.pad(back_down, ((0, size - over), (0, 0), (0, 0))))
            restrict = jnp.einsum('mk,mb->kb', basis, resid.reshape(size * size, n_rhs), precision=highest, preferred_element_type=jnp.float32)
            gathered = lax.all_gather(restrict, grid_axes, tiled=True)
            own_coef = matmul(own_map, gathered)
            return level_one + matmul(basis, own_coef).reshape(size, size, n_rhs)

        def global_dot(first, second):
            return lax.psum(jnp.sum(first * second, axis=(0, 1)), grid_axes)

        forcing_norm = jnp.sqrt(global_dot(forcing, forcing))
        solved = jnp.zeros_like(forcing)
        resid = forcing
        precond = schwarz(resid)
        direction = precond
        rz_dot = global_dot(resid, precond)
        norms = []
        for step in range(ITERS):
            image = apply_local(direction)
            alpha = rz_dot / global_dot(direction, image)
            solved = solved + alpha * direction
            resid = resid - alpha * image
            if step < ITERS - 1:
                precond = schwarz(resid)
                both = lax.psum(jnp.stack([jnp.sum(resid * precond, axis=(0, 1)), jnp.sum(resid * resid, axis=(0, 1))]), grid_axes)
                norms.append(jnp.sqrt(both[1]) / forcing_norm)
                direction = precond + (both[0] / rz_dot) * direction
                rz_dot = both[0]
            else:
                norms.append(jnp.sqrt(global_dot(resid, resid)) / forcing_norm)
        return solved, jnp.stack(norms)

    cell_spec = P(('batch', 'sx'), 'sy', None)
    sub_spec = P(('batch', 'sx', 'sy'), None, None)
    return jax.shard_map(body, mesh=mesh, in_specs=(cell_spec, P(('batch', 'sx'), 'sy'), sub_spec, sub_spec, P(('batch', 'sx', 'sy')), P('batch', None)), out_specs=(cell_spec, P('batch', None)), check_vma=False)
```

profile of v0, /device:TPU:0, one launch (start us, length us, event | category | flops | bytes accessed | tf_op | source)
XLA Modules:
  0.0 1333.2 jit_solution(11174843942741878743)
XLA Ops:
  6.2 3.7 collective-permute-start
  14.3 14.1 %all-reduce.32 = s32[16]{0:T(128)S(1)} all-reduce(s32[16]{0:T(128)S(1)} %dynamic-update-slice), channel_id=1, replica_groups=mesh['batch'=2,'sy'=4,'sx'=4] {'sx','sy'}, use_global_device_ids=true, to_apply=%add.32 | all-reduce | flops 16 | bytes 128
  31.8 31.0 %all_gather.28 = f32[128,256]{1,0:T(8,128)S(1)} all-gather(f32[8,256]{1,0:T(8,128)S(1)} %fusion.87), channel_id=1, replica_groups=mesh['batch'=2,'sy'=4,'sx'=4] {'sx','sy'}, dimensions={0}, use_global_device_ids=true | all-gather | bytes 139264 | tf_op jit(solution)/shard_map/all_gather | solution.py:93
  64.2 20.1 %compare_select_fusion.1 = s32[128]{0:T(128)S(1)} fusion(s32[]{:T(128)} %bitcast.44, s32[]{:T(128)} %bitcast.27, s32[]{:T(128)} %bitcast.45, s32[]{:T(128)} %bitcast.28, s32[]{:T(128)} %bitcast.46, s32[]{:T(128)} %bitcast.29, s32[]{:T(128)} %bitcast.47, s32[]{:T(128)} %bitcast.30, s32[]{:T(128)} %bitcast.48, s32[]{:T(128)} %bitcast.31, s32[]{:T(128)} %bitcast.50, ...), kind=kLoop, calls=%fused_computation.267 | loop fusion | flops 8320 | bytes 640 | tf_op jit(solution)/shard_map/jit(_where)/select_n | solution.py:59
  97.2 4.7 collective-permute-done.3
  102.1 11.9 fusion.14
  115.4 4.6 collective-permute-start.5
  124.9 3.0 collective-permute-start.7
  129.4 4.4 collective-permute-start.14
  139.9 3.4 collective-permute-done.13
  145.8 32.3 %all-reduce.34 = (f32[256]{0:T(256)S(1)}, f32[256]{0:T(256)S(1)}) all-reduce(f32[256]{0:T(256)S(1)} %get-tuple-element.3, f32[256]{0:T(256)S(1)} %get-tuple-element.4), channel_id=1, replica_groups=mesh['batch'=2,'sy'=4,'sx'=4] {'sx','sy'}, use_global_device_ids=true, to_apply=%region_2.3 | all-reduce | flops 512 | bytes 4096 | tf_op jit(solution)/shard_map/psum | solution.py:98
  182.1 5.4 collective-permute-done.17
  190.8 32.5 %all_gather.29 = f32[128,256]{1,0:T(8,128)S(1)} all-gather(f32[8,256]{1,0:T(8,128)S(1)} %convolution_bitcast_fusion.14), channel_id=1, replica_groups=mesh['batch'=2,'sy'=4,'sx'=4] {'sx','sy'}, dimensions={0}, use_global_device_ids=true | all-gather | bytes 139264 | tf_op jit(solution)/shard_map/all_gather | solution.py:93
  223.5 11.9 fusion.12
  236.8 4.6 collective-permute-start.21
  247.7 3.0 collective-permute-start.23
  255.8 33.4 %psum.128 = f32[2,256]{1,0:T(2,128)S(1)} all-reduce(f32[2,256]{1,0:T(2,128)S(1)} %pad_maximum_fusion.33), channel_id=1, replica_groups=mesh['batch'=2,'sy'=4,'sx'=4] {'sx','sy'}, use_global_device_ids=true, to_apply=%region_7.8 | all-reduce | flops 512 | bytes 4096 | tf_op jit(solution)/shard_map/psum | solution.py:114
  298.9 3.3 collective-permute-done.25
  303.9 32.3 %psum.129 = f32[256]{0:T(256)S(1)} all-reduce(f32[256]{0:T(256)S(1)} %get-tuple-element.35), channel_id=1, replica_groups=mesh['batch'=2,'sy'=4,'sx'=4] {'sx','sy'}, use_global_device_ids=true, to_apply=%region_9.10 | all-reduce | flops 256 | bytes 2048 | tf_op jit(solution)/shard_map/psum | solution.py:98
  340.6 5.1 collective-permute-done.29
  349.2 32.2 %all_gather.30 = f32[128,256]{1,0:T(8,128)S(1)} all-gather(f32[8,256]{1,0:T(8,128)S(1)} %convolution_bitcast_fusion.13), channel_id=1, replica_groups=mesh['batch'=2,'sy'=4,'sx'=4] {'sx','sy'}, dimensions={0}, use_global_device_ids=true | all-gather | bytes 139264 | tf_op jit(solution)/shard_map/all_gather | solution.py:93
  381.6 11.9 fusion.10
  394.9 4.6 collective-permute-start.33
  405.6 3.0 collective-permute-start.35
  415.0 33.4 %psum.130 = f32[2,256]{1,0:T(2,128)S(1)} all-reduce(f32[2,256]{1,0:T(2,128)S(1)} %pad_maximum_fusion.34), channel_id=1, replica_groups=mesh['batch'=2,'sy'=4,'sx'=4] {'sx','sy'}, use_global_device_ids=true, to_apply=%region_12.13 | all-reduce | flops 512 | bytes 4096 | tf_op jit(solution)/shard_map/psum | solution.py:114
  458.4 3.0 collective-permute-done.37
  463.2 32.3 %psum.131 = f32[256]{0:T(256)S(1)} all-reduce(f32[256]{0:T(256)S(1)} %get-tuple-element.33), channel_id=1, replica_groups=mesh['batch'=2,'sy'=4,'sx'=4] {'sx','sy'}, use_global_device_ids=true, to_apply=%region_14.15 | all-reduce | flops 256 | bytes 2048 | tf_op jit(solution)/shard_map/psum | solution.py:98
  499.8 5.1 collective-permute-done.41
  508.4 32.3 %all_gather.31 = f32[128,256]{1,0:T(8,128)S(1)} all-gather(f32[8,256]{1,0:T(8,128)S(1)} %convolution_bitcast_fusion.12), channel_id=1, replica_groups=mesh['batch'=2,'sy'=4,'sx'=4] {'sx','sy'}, dimensions={0}, use_global_device_ids=true | all-gather | bytes 139264 | tf_op jit(solution)/shard_map/all_gather | solution.py:93
  540.9 11.9 fusion.8
  554.2 4.6 collective-permute-start.45
  564.9 3.0 collective-permute-start.47
  574.6 33.4 %psum.132 = f32[2,256]{1,0:T(2,128)S(1)} all-reduce(f32[2,256]{1,0:T(2,128)S(1)} %pad_maximum_fusion.35), channel_id=1, replica_groups=mesh['batch'=2,'sy'=4,'sx'=4] {'sx','sy'}, use_global_device_ids=true, to_apply=%region_17.18 | all-reduce | flops 512 | bytes 4096 | tf_op jit(solution)/shard_map/psum | solution.py:114
  622.7 32.3 %psum.133 = f32[256]{0:T(256)S(1)} all-reduce(f32[256]{0:T(256)S(1)} %get-tuple-element.31), channel_id=1, replica_groups=mesh['batch'=2,'sy'=4,'sx'=4] {'sx','sy'}, use_global_device_ids=true, to_apply=%region_19.20 | all-reduce | flops 256 | bytes 2048 | tf_op jit(solution)/shard_map/psum | solution.py:98
  659.3 5.1 collective-permute-done.53
  667.9 32.5 %all_gather.32 = f32[128,256]{1,0:T(8,128)S(1)} all-gather(f32[8,256]{1,0:T(8,128)S(1)} %convolution_bitcast_fusion.11), channel_id=1, replica_groups=mesh['batch'=2,'sy'=4,'sx'=4] {'sx','sy'}, dimensions={0}, use_global_device_ids=true | all-gather | bytes 139264 | tf_op jit(solution)/shard_map/all_gather | solution.py:93
  700.6 11.9 fusion.6
  713.9 4.6 collective-permute-start.57
  724.6 3.0 collective-permute-start.59
  734.4 33.4 %psum.134 = f32[2,256]{1,0:T(2,128)S(1)} all-reduce(f32[2,256]{1,0:T(2,128)S(1)} %pad_maximum_fusion.36), channel_id=1, replica_groups=mesh['batch'=2,'sy'=4,'sx'=4] {'sx','sy'}, use_global_device_ids=true, to_apply=%region_22.23 | all-reduce | flops 512 | bytes 4096 | tf_op jit(solution)/shard_map/psum | solution.py:114
  782.7 32.3 %psum.135 = f32[256]{0:T(256)S(1)} all-reduce(f32[256]{0:T(256)S(1)} %get-tuple-element.29), channel_id=1, replica_groups=mesh['batch'=2,'sy'=4,'sx'=4] {'sx','sy'}, use_global_device_ids=true, to_apply=%region_24.25 | all-reduce | flops 256 | bytes 2048 | tf_op jit(solution)/shard_map/psum | solution.py:98
  819.4 5.1 collective-permute-done.65
  828.0 32.2 %all_gather.33 = f32[128,256]{1,0:T(8,128)S(1)} all-gather(f32[8,256]{1,0:T(8,128)S(1)} %convolution_bitcast_fusion.10), channel_id=1, replica_groups=mesh['batch'=2,'sy'=4,'sx'=4] {'sx','sy'}, dimensions={0}, use_global_device_ids=true | all-gather | bytes 139264 | tf_op jit(solution)/shard_map/all_gather | solution.py:93
  860.4 11.9 fusion.4
  873.7 4.6 collective-permute-start.69
  884.4 3.0 collective-permute-start.71
  894.2 33.4 %psum.136 = f32[2,256]{1,0:T(2,128)S(1)} all-reduce(f32[2,256]{1,0:T(2,128)S(1)} %pad_maximum_fusion.37), channel_id=1, replica_groups=mesh['batch'=2,'sy'=4,'sx'=4] {'sx','sy'}, use_global_device_ids=true, to_apply=%region_27.28 | all-reduce | flops 512 | bytes 4096 | tf_op jit(solution)/shard_map/psum | solution.py:114
  942.6 32.3 %psum.137 = f32[256]{0:T(256)S(1)} all-reduce(f32[256]{0:T(256)S(1)} %get-tuple-element.27), channel_id=1, replica_groups=mesh['batch'=2,'sy'=4,'sx'=4] {'sx','sy'}, use_global_device_ids=true, to_apply=%region_29.30 | all-reduce | flops 256 | bytes 2048 | tf_op jit(solution)/shard_map/psum | solution.py:98
  979.3 5.1 collective-permute-done.77
  987.9 32.3 %all_gather.34 = f32[128,256]{1,0:T(8,128)S(1)} all-gather(f32[8,256]{1,0:T(8,128)S(1)} %convolution_bitcast_fusion.9), channel_id=1, replica_groups=mesh['batch'=2,'sy'=4,'sx'=4] {'sx','sy'}, dimensions={0}, use_global_device_ids=true | all-gather | bytes 139264 | tf_op jit(solution)/shard_map/all_gather | solution.py:93
  1020.3 11.9 fusion.2
  1033.6 4.6 collective-permute-start.81
  1044.3 3.0 collective-permute-start.83
  1054.1 33.9 %psum.138 = f32[2,256]{1,0:T(2,128)} all-reduce(f32[2,256]{1,0:T(2,128)S(1)} %pad_maximum_fusion.38), channel_id=1, replica_groups=mesh['batch'=2,'sy'=4,'sx'=4] {'sx','sy'}, use_global_device_ids=true, to_apply=%region_32.33 | all-reduce | flops 512 | bytes 4096 | tf_op jit(solution)/shard_map/psum | solution.py:114
  1103.8 32.3 %psum.139 = f32[256]{0:T(256)S(1)} all-reduce(f32[256]{0:T(256)S(1)} %get-tuple-element.25), channel_id=1, replica_groups=mesh['batch'=2,'sy'=4,'sx'=4] {'sx','sy'}, use_global_device_ids=true, to_apply=%region_34.35 | all-reduce | flops 256 | bytes 2048 | tf_op jit(solution)/shard_map/psum | solution.py:98
  1140.4 5.1 collective-permute-done.89
  1149.0 32.3 %all_gather.35 = f32[128,256]{1,0:T(8,128)S(1)} all-gather(f32[8,256]{1,0:T(8,128)S(1)} %convolution_bitcast_fusion.8), channel_id=1, replica_groups=mesh['batch'=2,'sy'=4,'sx'=4] {'sx','sy'}, dimensions={0}, use_global_device_ids=true | all-gather | bytes 139264 | tf_op jit(solution)/shard_map/all_gather | solution.py:93
  1181.6 11.9 fusion
  1194.8 4.6 collective-permute-start.93
  1205.5 3.0 collective-permute-start.95
  1215.4 33.9 %psum.140 = f32[2,256]{1,0:T(2,128)} all-reduce(f32[2,256]{1,0:T(2,128)S(1)} %pad_maximum_fusion.39), channel_id=1, replica_groups=mesh['batch'=2,'sy'=4,'sx'=4] {'sx','sy'}, use_global_device_ids=true, to_apply=%region_37.38 | all-reduce | flops 512 | bytes 4096 | tf_op jit(solution)/shard_map/psum | solution.py:114
  1265.0 32.3 %psum.141 = f32[256]{0:T(256)S(1)} all-reduce(f32[256]{0:T(256)S(1)} %get-tuple-element.23), channel_id=1, replica_groups=mesh['batch'=2,'sy'=4,'sx'=4] {'sx','sy'}, use_global_device_ids=true, to_apply=%region_39.40 | all-reduce | flops 256 | bytes 2048 | tf_op jit(solution)/shard_map/psum | solution.py:98
  1297.4 5.1 multiply_reduce_fusion
  1302.5 29.7 %all-reduce.33 = (f32[256]{0:T(256)S(1)}, f32[256]{0:T(256)S(1)}) all-reduce(f32[256]{0:T(256)S(1)} %copy-done.25, f32[256]{0:T(256)S(1)} %get-tuple-element.201), channel_id=1, replica_groups=mesh['batch'=2,'sy'=4,'sx'=4] {'sx','sy'}, use_global_device_ids=true, to_apply=%region_41.42 | all-reduce | flops 512 | bytes 4096 | tf_op jit(solution)/shard_map/psum | solution.py:98
  (435 shorter events, 296.0 us)
Async XLA Ops:
  1.4 85.6 %collective-permute-start.9 = (f32[1,32]{1,0:T(1,128)S(1)}, f32[1,32]{1,0:T(1,128)S(1)}, u32[]{:S(2)}, u32[]{:S(2)}) collective-permute-start(f32[1,32]{1,0:T(1,128)S(1)} %slice.519), channel_id=1, source_target_pairs={{1,0},{2,1},{3,2},{5,4},{6,5},{7,6},{9,8},{10,9},{11,10},{13,12},{... | collective-permute-start | bytes 392 | tf_op jit(solution)/shard_map/ppermute | solution.py:40
  2.6 85.6 %collective-permute-start.11 = (f32[32,1]{1,0:T(8,128)}, f32[32,1]{1,0:T(8,128)S(1)}, u32[]{:S(2)}, u32[]{:S(2)}) collective-permute-start(f32[32,1]{1,0:T(8,128)} %bitcast.415), channel_id=1, source_target_pairs={{4,0},{8,4},{12,8},{5,1},{9,5},{13,9},{6,2},{10,6},{14,10},{7,3},{... | collective-permute-start | bytes 392 | tf_op jit(solution)/shard_map/ppermute | solution.py:42
  4.9 86.1 %collective-permute-start.1 = (f32[4,32,256]{2,1,0:T(8,128)S(1)}, f32[4,32,256]{2,1,0:T(8,128)S(1)}, u32[]{:S(2)}, u32[]{:S(2)}) collective-permute-start(f32[4,32,256]{2,1,0:T(8,128)S(1)} %get-tuple-element.169), channel_id=1, source_target_pairs={{1,0},{2,1},{3,2},{5,4},{6,5},{7,6},{9,8},{10,9},{11,10},{13,12},{... | collective-permute-start | bytes 393224 | tf_op jit(solution)/shard_map/ppermute | solution.py:80
  6.2 84.6 %collective-permute-start = (f32[4,32,256]{2,1,0:T(8,128)S(1)}, f32[4,32,256]{2,1,0:T(8,128)S(1)}, u32[]{:S(2)}, u32[]{:S(2)}) collective-permute-start(f32[4,32,256]{2,1,0:T(8,128)S(1)} %get-tuple-element.170), channel_id=1, source_target_pairs={{0,1},{1,2},{2,3},{4,5},{5,6},{6,7},{8,9},{9,10},{10,11},{12,13},{... | collective-permute-start | bytes 393224 | tf_op jit(solution)/shard_map/ppermute | solution.py:79
  86.9 33.0 %collective-permute-start.8 = (f32[1,32]{1,0:T(1,128)S(1)}, f32[1,32]{1,0:T(1,128)S(1)}, u32[]{:S(2)}, u32[]{:S(2)}) collective-permute-start(f32[1,32]{1,0:T(1,128)S(1)} %get-tuple-element.178), channel_id=1, source_target_pairs={{0,1},{1,2},{2,3},{4,5},{5,6},{6,7},{8,9},{9,10},{10,11},{12,13},{... | collective-permute-start | bytes 392 | tf_op jit(solution)/shard_map/ppermute | solution.py:39
  93.0 8.9 collective-permute-start.3
  114.1 8.1 collective-permute-start.4
  115.4 8.0 collective-permute-start.5
  129.4 10.1 collective-permute-start.14
  180.8 6.7 collective-permute-start.17
  187.6 35.7 %collective-permute-start.18 = (f32[40,4,256]{2,1,0:T(4,128)S(1)}, f32[40,4,256]{2,1,0:T(4,128)S(1)}, u32[]{:S(2)}, u32[]{:S(2)}) collective-permute-start(f32[40,4,256]{2,1,0:T(4,128)S(1)} %get-tuple-element.85), channel_id=1, source_target_pairs={{0,4},{4,8},{8,12},{1,5},{5,9},{9,13},{2,6},{6,10},{10,14},{3,7},{... | collective-permute-start | bytes 491528 | tf_op jit(solution)/shard_map/ppermute | solution.py:82
  188.9 34.4 %collective-permute-start.19 = (f32[40,4,256]{2,1,0:T(4,128)S(1)}, f32[40,4,256]{2,1,0:T(4,128)S(1)}, u32[]{:S(2)}, u32[]{:S(2)}) collective-permute-start(f32[40,4,256]{2,1,0:T(4,128)S(1)} %get-tuple-element.86), channel_id=1, source_target_pairs={{4,0},{8,4},{12,8},{5,1},{9,5},{13,9},{6,2},{10,6},{14,10},{7,3},{... | collective-permute-start | bytes 491528 | tf_op jit(solution)/shard_map/ppermute | solution.py:83
  235.5 7.7 collective-permute-start.20
  236.8 7.5 collective-permute-start.21
  246.4 7.9 collective-permute-start.22
  247.7 6.6 collective-permute-start.23
  295.7 6.5 collective-permute-start.25
  339.3 6.4 collective-permute-start.29
  345.8 35.6 %collective-permute-start.30 = (f32[40,4,256]{2,1,0:T(4,128)S(1)}, f32[40,4,256]{2,1,0:T(4,128)S(1)}, u32[]{:S(2)}, u32[]{:S(2)}) collective-permute-start(f32[40,4,256]{2,1,0:T(4,128)S(1)} %get-tuple-element.81), channel_id=1, source_target_pairs={{0,4},{4,8},{8,12},{1,5},{5,9},{9,13},{2,6},{6,10},{10,14},{3,7},{... | collective-permute-start | bytes 491528 | tf_op jit(solution)/shard_map/ppermute | solution.py:82
  347.3 34.1 %collective-permute-start.31 = (f32[40,4,256]{2,1,0:T(4,128)S(1)}, f32[40,4,256]{2,1,0:T(4,128)S(1)}, u32[]{:S(2)}, u32[]{:S(2)}) collective-permute-start(f32[40,4,256]{2,1,0:T(4,128)S(1)} %get-tuple-element.82), channel_id=1, source_target_pairs={{4,0},{8,4},{12,8},{5,1},{9,5},{13,9},{6,2},{10,6},{14,10},{7,3},{... | collective-permute-start | bytes 491528 | tf_op jit(solution)/shard_map/ppermute | solution.py:83
  393.6 7.2 collective-permute-start.32
  394.9 7.4 collective-permute-start.33
  404.3 8.9 collective-permute-start.34
  405.6 7.6 collective-permute-start.35
  455.2 6.2 collective-permute-start.37
  498.5 6.4 collective-permute-start.41
  505.0 35.7 %collective-permute-start.42 = (f32[40,4,256]{2,1,0:T(4,128)S(1)}, f32[40,4,256]{2,1,0:T(4,128)S(1)}, u32[]{:S(2)}, u32[]{:S(2)}) collective-permute-start(f32[40,4,256]{2,1,0:T(4,128)S(1)} %get-tuple-element.77), channel_id=1, source_target_pairs={{0,4},{4,8},{8,12},{1,5},{5,9},{9,13},{2,6},{6,10},{10,14},{3,7},{... | collective-permute-start | bytes 491528 | tf_op jit(solution)/shard_map/ppermute | solution.py:82
  506.5 34.2 %collective-permute-start.43 = (f32[40,4,256]{2,1,0:T(4,128)S(1)}, f32[40,4,256]{2,1,0:T(4,128)S(1)}, u32[]{:S(2)}, u32[]{:S(2)}) collective-permute-start(f32[40,4,256]{2,1,0:T(4,128)S(1)} %get-tuple-element.78), channel_id=1, source_target_pairs={{4,0},{8,4},{12,8},{5,1},{9,5},{13,9},{6,2},{10,6},{14,10},{7,3},{... | collective-permute-start | bytes 491528 | tf_op jit(solution)/shard_map/ppermute | solution.py:83
  552.9 7.2 collective-permute-start.44
  554.2 7.4 collective-permute-start.45
  563.6 8.9 collective-permute-start.46
  564.9 7.6 collective-permute-start.47
  658.0 6.4 collective-permute-start.53
  664.5 35.9 %collective-permute-start.54 = (f32[40,4,256]{2,1,0:T(4,128)S(1)}, f32[40,4,256]{2,1,0:T(4,128)S(1)}, u32[]{:S(2)}, u32[]{:S(2)}) collective-permute-start(f32[40,4,256]{2,1,0:T(4,128)S(1)} %get-tuple-element.73), channel_id=1, source_target_pairs={{0,4},{4,8},{8,12},{1,5},{5,9},{9,13},{2,6},{6,10},{10,14},{3,7},{... | collective-permute-start | bytes 491528 | tf_op jit(solution)/shard_map/ppermute | solution.py:82
  666.0 34.4 %collective-permute-start.55 = (f32[40,4,256]{2,1,0:T(4,128)S(1)}, f32[40,4,256]{2,1,0:T(4,128)S(1)}, u32[]{:S(2)}, u32[]{:S(2)}) collective-permute-start(f32[40,4,256]{2,1,0:T(4,128)S(1)} %get-tuple-element.74), channel_id=1, source_target_pairs={{4,0},{8,4},{12,8},{5,1},{9,5},{13,9},{6,2},{10,6},{14,10},{7,3},{... | collective-permute-start | bytes 491528 | tf_op jit(solution)/shard_map/ppermute | solution.py:83
  712.6 7.2 collective-permute-start.56
  713.9 7.4 collective-permute-start.57
  723.3 8.9 collective-permute-start.58
  724.6 7.6 collective-permute-start.59
  774.9 6.2 collective-permute-start.61
  818.1 6.4 collective-permute-start.65
  824.6 35.6 %collective-permute-start.66 = (f32[40,4,256]{2,1,0:T(4,128)S(1)}, f32[40,4,256]{2,1,0:T(4,128)S(1)}, u32[]{:S(2)}, u32[]{:S(2)}) collective-permute-start(f32[40,4,256]{2,1,0:T(4,128)S(1)} %get-tuple-element.69), channel_id=1, source_target_pairs={{0,4},{4,8},{8,12},{1,5},{5,9},{9,13},{2,6},{6,10},{10,14},{3,7},{... | collective-permute-start | bytes 491528 | tf_op jit(solution)/shard_map/ppermute | solution.py:82
  826.1 34.1 %collective-permute-start.67 = (f32[40,4,256]{2,1,0:T(4,128)S(1)}, f32[40,4,256]{2,1,0:T(4,128)S(1)}, u32[]{:S(2)}, u32[]{:S(2)}) collective-permute-start(f32[40,4,256]{2,1,0:T(4,128)S(1)} %get-tuple-element.70), channel_id=1, source_target_pairs={{4,0},{8,4},{12,8},{5,1},{9,5},{13,9},{6,2},{10,6},{14,10},{7,3},{... | collective-permute-start | bytes 491528 | tf_op jit(solution)/shard_map/ppermute | solution.py:83
  872.4 7.2 collective-permute-start.68
  873.7 7.4 collective-permute-start.69
  883.1 8.9 collective-permute-start.70
  884.4 7.6 collective-permute-start.71
  934.7 6.2 collective-permute-start.73
  978.0 6.4 collective-permute-start.77
  984.4 35.7 %collective-permute-start.78 = (f32[40,4,256]{2,1,0:T(4,128)S(1)}, f32[40,4,256]{2,1,0:T(4,128)S(1)}, u32[]{:S(2)}, u32[]{:S(2)}) collective-permute-start(f32[40,4,256]{2,1,0:T(4,128)S(1)} %get-tuple-element.65), channel_id=1, source_target_pairs={{0,4},{4,8},{8,12},{1,5},{5,9},{9,13},{2,6},{6,10},{10,14},{3,7},{... | collective-permute-start | bytes 491528 | tf_op jit(solution)/shard_map/ppermute | solution.py:82
  985.9 34.2 %collective-permute-start.79 = (f32[40,4,256]{2,1,0:T(4,128)S(1)}, f32[40,4,256]{2,1,0:T(4,128)S(1)}, u32[]{:S(2)}, u32[]{:S(2)}) collective-permute-start(f32[40,4,256]{2,1,0:T(4,128)S(1)} %get-tuple-element.66), channel_id=1, source_target_pairs={{4,0},{8,4},{12,8},{5,1},{9,5},{13,9},{6,2},{10,6},{14,10},{7,3},{... | collective-permute-start | bytes 491528 | tf_op jit(solution)/shard_map/ppermute | solution.py:83
  1032.3 7.2 collective-permute-start.80
  1033.6 7.4 collective-permute-start.81
  1043.1 8.9 collective-permute-start.82
  1044.3 7.6 collective-permute-start.83
  1095.9 6.2 collective-permute-start.85
  1139.1 6.4 collective-permute-start.89
  1145.6 35.7 %collective-permute-start.90 = (f32[40,4,256]{2,1,0:T(4,128)S(1)}, f32[40,4,256]{2,1,0:T(4,128)S(1)}, u32[]{:S(2)}, u32[]{:S(2)}) collective-permute-start(f32[40,4,256]{2,1,0:T(4,128)S(1)} %get-tuple-element.61), channel_id=1, source_target_pairs={{0,4},{4,8},{8,12},{1,5},{5,9},{9,13},{2,6},{6,10},{10,14},{3,7},{... | collective-permute-start | bytes 491528 | tf_op jit(solution)/shard_map/ppermute | solution.py:82
  1147.1 34.2 %collective-permute-start.91 = (f32[40,4,256]{2,1,0:T(4,128)S(1)}, f32[40,4,256]{2,1,0:T(4,128)S(1)}, u32[]{:S(2)}, u32[]{:S(2)}) collective-permute-start(f32[40,4,256]{2,1,0:T(4,128)S(1)} %get-tuple-element.62), channel_id=1, source_target_pairs={{4,0},{8,4},{12,8},{5,1},{9,5},{13,9},{6,2},{10,6},{14,10},{7,3},{... | collective-permute-start | bytes 491528 | tf_op jit(solution)/shard_map/ppermute | solution.py:83
  1193.5 7.2 collective-permute-start.92
  1194.8 7.4 collective-permute-start.93
  1204.2 8.9 collective-permute-start.94
  1205.5 7.6 collective-permute-start.95
  1257.1 6.2 collective-permute-start.97
  (70 other events, 995.5 us)
where the time goes:
time: 1350 us; the launch traced here: 1330 us
  blocking collectives  794 us (59%)
  starting transfers between devices  180 us (13%)
  matrix products  118 us (9%)
  waiting for transfers between devices  103 us (8%)
  other arithmetic  85.5 us (6%)
  local copies, waits for them, and re-layouts  48.7 us (4%)
    psum x9, blocking collectives, global_dot(): return lax.psum(jnp.sum(first * second, axis=(0, 1)), grid_axes)  288 us
    all_gather x8, blocking collectives, schwarz(): gathered = lax.all_gather(restrict, grid_axes, tiled=True)  257 us
    psum x7, blocking collectives, body(): lax.psum(jnp.stack([jnp.sum(resid * precond, axis=(0, 1)), jnp.sum(resid...  235 us
    dot_general x26, matrix products, matmul(): jnp.dot(first, second, precision=highest, preferred_element_type=jnp.floa...  112 us
    ppermute x8, starting transfers between devices, schwarz(): back_right = lax.ppermute(local[:, size + over:], 'sy', to_right)  36.4 us
    ppermute x8, waiting for transfers between devices, schwarz(): from_bottom = lax.ppermute(resid[:over], 'sx', to_above)  36 us
  transfers between devices with their start and end apart: 100, of which 42 were waited for; matrix products, arithmetic and copies ran while one was open for 6% of the time, Pallas kernels for 0%

commit v1 on v0

v1 whole, which is shorter than its diff:
```python
import jax
import jax.numpy as jnp
from jax import lax
from jax.experimental import pallas as pl
from jax.experimental.pallas import tpu as pltpu
from jax.sharding import PartitionSpec as P

ITERS = 8
M = 32
D = 4
ME = M + 2 * D
NE = ME * ME
SUB = 8
LANES = 128
TILE = 256
KT = NE // TILE
KM = KT * TILE
REM = NE - KM
ROWS = 10
CHUNK = ROWS * ME
BT = 16
NL = NE + 2 * BT
KMAX = 8
GRID = 128
LOW = M + SUB + D
WIDE = M + 2 * SUB
OWN = D + 1
STRIP = 9
EDGE = STRIP + 2
MESH = pl.DeviceIdType.MESH
HI = lax.Precision.HIGHEST
F32 = jnp.float32
BF16 = jnp.bfloat16
HALVES = (0, 1)
PIECES = (0, 1, 2)
FAR = (1, 2, 3)
LAST = FAR[-1]
SIDE = FAR[-1] + 1


def lanes(h):
    return slice(LANES * h, LANES * (h + 1))


def tile(k):
    return slice(TILE * k, TILE * (k + 1))


def mult(v, n=BT):
    return v if isinstance(v, int) else pl.multiple_of(v, n)


def row(v, k):
    return v[k:k + 1]


def wide(v):
    return jnp.broadcast_to(v, (SUB, LANES))


def colsum(v):
    return jnp.sum(v, axis=0, keepdims=True)


def each(copies, what):
    for c in copies:
        getattr(c, what)()


def split3(v):
    hi = v.astype(BF16)
    rest = v - hi.astype(F32)
    mid = rest.astype(BF16)
    low = (rest - mid.astype(F32)).astype(BF16)
    return hi, mid, low


def solve_kernel(f_hbm, aux_hbm, inv_hbm, bt_ref, cinv_ref, cnt_ref, x_hbm, nrm_ref,
                 S48, L, Lr, stage, X, Xr, T, TE, z, p, r, l, x, Q, Ey, W5, Ecat, RE,
               V, HB, HE, HP, PK, G1a, G2a, G1b, G2b, G1d, G2d, Ccat, cr, wr, cst, pqs,
               ld_sem, own_sem, h0_s, h0_r, v0_s, v0_r, v_s, v_r, hm_s, hm_r,
               a1_s, a1_r, a2_s, a2_r, b1_s, b1_r, b2_s, b2_r, d1_s, d1_r, d2_s, d2_r, out_sem):
    sx = lax.axis_index("sx")
    sy = lax.axis_index("sy")
    left, right = {"sy": sy - 1}, {"sy": sy + 1}
    has_left, has_right = sy > 0, sy < LAST
    has = (sx > 0, sx < LAST)
    near = lax.rem(sx, 2)
    inner = (sx > 0) & (sx < LAST)

    def rc(src, dst, s, q, dev):
        return pltpu.make_async_remote_copy(src, dst, s, q, device_id=dev, device_id_type=MESH)

    own = pl.ds(OWN, M)
    inv_cp = [pltpu.make_async_copy(inv_hbm.at[pl.ds(CHUNK * c, CHUNK)], stage.at[c], ld_sem.at[c]) for c in range(SIDE)]
    own_cp = [pltpu.make_async_copy(f_hbm.at[:, :, pl.ds(LANES * h, LANES)], S48.at[h, own, pl.ds(SUB, M)], own_sem.at[h]) for h in HALVES]
    own_cp += [pltpu.make_async_copy(aux_hbm.at[h], S48.at[2 + h, own, pl.ds(SUB, M)], own_sem.at[2 + h]) for h in HALVES]
    each(own_cp, "start")
    each(inv_cp, "start")
    zrow = jnp.zeros((SIDE, OWN, WIDE, LANES), F32)
    S48[:, 0:OWN] = zrow
    S48[:, OWN + M:] = zrow
    zcol = jnp.zeros((SIDE, M, SUB, LANES), F32)
    S48[:, OWN:OWN + M, 0:SUB] = zcol
    S48[:, OWN:OWN + M, ME:] = zcol
    for b in (V, HB, HE, HP):
        b[...] = jnp.zeros(b.shape, F32)

    bar = pltpu.get_barrier_semaphore()
    for d in FAR:
        pl.semaphore_signal(bar, inc=1, device_id={"sx": lax.rem(sx + d, SIDE)}, device_id_type=MESH)
        pl.semaphore_signal(bar, inc=1, device_id={"sy": lax.rem(sy + d, SIDE)}, device_id_type=MESH)
    pl.semaphore_wait(bar, 2 * LAST)

    def first_copies(G1, s, q):
        return [rc(G1.at[sy], G1.at[sy], s.at[d - 1], q.at[d - 1], {"sy": lax.rem(sy + d, SIDE)}) for d in FAR]

    def second_copies(src, G2, s, q):
        return [rc(src, G2.at[sx], s.at[d - 1], q.at[d - 1], {"sx": lax.rem(sx + d, SIDE)}) for d in FAR]

    a1 = first_copies(G1a, a1_s, a1_r)
    a2 = second_copies(G1a, G2a, a2_s, a2_r)
    b1 = first_copies(G1b, b1_s, b1_r)
    b2 = second_copies(G2b.at[sx], G2b, b2_s, b2_r)
    d1 = first_copies(G1d, d1_s, d1_r)
    d2 = second_copies(G2d.at[sx], G2d, d2_s, d2_r)
    mine_y, mine_x = pl.ds(sy, 1), pl.ds(sx, 1)

    def half_sum(G1, G2, one, two):
        each(one, "wait")
        G2[mine_x] = jnp.sum(G1[...], axis=0, keepdims=True)
        each(two, "start")

    def full_sum(G2, two):
        each(two, "wait")
        return jnp.sum(G2[...], axis=0)

    G1b[mine_y] = jnp.broadcast_to(cnt_ref[...], (1, 2, SUB, LANES))
    each(b1, "start")

    each(own_cp, "wait")
    h0l = rc(S48.at[:, own, pl.ds(SUB, SUB)], S48.at[:, own, pl.ds(ME, SUB)], h0_s.at[0], h0_r.at[0], left)
    h0r = rc(S48.at[:, own, pl.ds(M, SUB)], S48.at[:, own, pl.ds(0, SUB)], h0_s.at[1], h0_r.at[1], right)
    v0 = [rc(S48.at[:, pl.ds(OWN, OWN)], S48.at[:, pl.ds(OWN + M, OWN)], v0_s.at[0], v0_r.at[1], {"sx": sx - 1}),
          rc(S48.at[:, pl.ds(M, OWN)], S48.at[:, pl.ds(0, OWN)], v0_s.at[1], v0_r.at[0], {"sx": sx + 1})]
    v0_in = [rc(S48.at[:, pl.ds(0, OWN)], S48.at[:, pl.ds(0, OWN)], v0_s.at[e], v0_r.at[e], left) for e in HALVES]
    pl.when(has_left)(h0l.start)
    pl.when(has_right)(h0r.start)

    for b in (p, z, r, l, x, T):
        def zero(i, c, b=b):
            b[:, pl.ds(i, 1)] = jnp.zeros((2, 1, ME, LANES), F32)
            return c
        lax.fori_loop(0, b.shape[1], zero, 0)
    Xr[...] = jnp.zeros(Xr.shape, BF16)
    for b in (cr, wr, cst, pqs, nrm_ref):
        b[...] = jnp.zeros(b.shape, F32)

    def put_l(v, rows):
        one, two, three = split3(v)
        rest = []
        for k, piece in enumerate((one, two, three)):
            L[rows, KM * k:KM * (k + 1)] = piece[:, 0:KM]
            rest.append(piece[:, KM:].astype(F32))
        twice = jnp.concatenate(rest[0:2], axis=1).astype(BF16)
        Lr[rows, lanes(0)] = twice
        Lr[rows, lanes(1)] = twice
        Lr[rows, lanes(2)] = jnp.concatenate([rest[0], rest[2]], axis=1).astype(BF16)
        Lr[rows, lanes(LAST)] = jnp.zeros(twice.shape, BF16)

    for at in (0, LAST * CHUNK + BT):
        put_l(bt_ref[...], pl.ds(at, BT))
    half_sum(G1b, G2b, b1, b2)

    def split_inv(c):
        inv_cp[c].wait()

        def body(k, carry):
            put_l(stage[c, pl.ds(mult(BT * k), BT), :], pl.ds(mult(CHUNK * c + BT * (c // LAST + 1) + BT * k), BT))
            return carry
        lax.fori_loop(0, CHUNK // BT, body, 0)

    split_inv(0)
    split_inv(1)
    pl.when(has_left)(h0l.wait_send)
    pl.when(has_right)(h0r.wait_send)
    pl.when(has_right)(h0l.wait_recv)
    pl.when(has_left)(h0r.wait_recv)
    for e in HALVES:
        pl.when(has[e])(v0[e].start)
    split_inv(2)
    split_inv(LAST)

    def dot(a, b):
        return jnp.dot(a, b, preferred_element_type=F32)

    def dot_pieces(lhs, v):
        y1, y2, y3 = split3(v)
        total = 0.0
        for n, two in enumerate(((y1, y1), (y2, y2), (y3, y1))):
            total = total + dot(lhs(LANES * (n // 2)), jnp.concatenate(two, axis=0))
        return total

    cnt = full_sum(G2b, b2)[0]
    lane = lax.broadcasted_iota(jnp.int32, (SUB, LANES), 1)
    starts = cnt
    for d in (KMAX, 2 * KMAX, D * KMAX, SUB * KMAX):
        starts = starts + jnp.where(lane >= d, pltpu.roll(starts, d, 1), 0.0)
    starts = starts - cnt
    col = (lane % KMAX).astype(F32)
    target = jnp.where(col < cnt, starts + col, -1.0)
    half = cinv_ref.shape[0]
    pick = jnp.where(lax.broadcasted_iota(jnp.int32, (half, LANES), 0).astype(F32) == row(target, 0), 1.0, 0.0)

    def rhs_of(parts):
        v = jnp.concatenate(parts + [jnp.zeros_like(parts[0])], axis=0)
        return v.astype(BF16)

    def lhs_of(parts):
        v = jnp.concatenate(parts + [jnp.zeros_like(parts[0])], axis=1)
        return v.astype(BF16)

    def as_f32(v):
        return [piece.astype(F32) for piece in split3(v)]
    spread = dot(lhs_of(as_f32(cinv_ref[...])), rhs_of([pick] * len(PIECES)))
    spread = dot(lhs_of([pick.T] * len(PIECES)), rhs_of(as_f32(spread)))

    def put_middle(ref, rows, v):
        for k, piece in zip((1, 0, 2), split3(v)):
            ref[rows, lanes(k)] = piece
    put_middle(Ccat, pl.ds(0, LANES), spread)

    for e in HALVES:
        pl.when(has[e])(v0[e].wait_send)
        pl.when(has[e])(v0_in[e].wait_recv)

    jcol = lax.broadcasted_iota(jnp.int32, (ME, LANES), 0)
    gj = sy * M + jcol - D
    in_col = (gj >= 0) & (gj < GRID)

    def shifted(v, k=D):
        return pltpu.roll(v, WIDE - k, 0)[0:ME]

    def weights(i, c):
        gi = sx * M + i - D
        ok = in_col & (gi >= 0) & (gi < GRID)
        here = S48[LAST, i + 1]
        kc = shifted(here)

        def pair(other, inside):
            both = ok & inside
            w = jnp.where(both, 2.0 * kc * other / jnp.where(both, kc + other, 1.0), 0.0)
            return w, jnp.where(ok & jnp.logical_not(inside), kc, w)
        edges = (pair(shifted(S48[LAST, i]), ok & (gi > 0)), pair(shifted(S48[LAST, i + 2]), ok & (gi < GRID - 1)),
                 pair(shifted(here, D - 1), gj > 0), pair(shifted(here, D + 1), gj < GRID - 1))
        total = 0.0
        for k, (w, d) in enumerate(edges):
            W5[k, i] = w
            total = total + d
        W5[SIDE, i] = total
        return c
    lax.fori_loop(0, ME, weights, 0)

    for i in range(ME):
        RE[0, i:i + 1] = S48[2, i + 1, D - 1:D]
        RE[1, i:i + 1] = S48[2, i + 1, LOW:LOW + 1]

    def pair_of(two, k):
        return jnp.concatenate(two, axis=0), pl.ds(mult(2 * ME * k), 2 * ME)

    def basis_rows(k, c):
        v, rows = pair_of([shifted(S48[2, 2 * k]), shifted(S48[2, 2 * k + 1])], k)
        put_middle(Ecat, rows, v)
        return c
    lax.fori_loop(0, LOW // 2 - 1, basis_rows, 0)
    v, rows = pair_of([RE[0], RE[1]], LOW // 2 - 1)
    put_middle(Ecat, rows, v)

    def put_x(two, h, k):
        v, rows = pair_of(two, k)
        pieces = split3(v)
        if isinstance(k, int) and k == ME // 2 - 1:
            n = KM - 2 * ME * k
            for j, piece in enumerate(pieces):
                X[j, KM - n:KM, lanes(h)] = piece[0:n]
            for slot, j in enumerate((0, 0, 1, 1, 2, 0)):
                Xr[REM * slot:REM * (slot + 1), lanes(h)] = pieces[j][n:]
        else:
            for j, piece in enumerate(pieces):
                X[j, rows, lanes(h)] = piece

    def first_rows(k, c):
        for h in HALVES:
            two = [shifted(S48[h, 2 * k + 1 + j]) for j in HALVES]
            for j in HALVES:
                Q[h, 2 * k + 1 + j] = two[j]
            put_x(two, h, k)
        return c
    lax.fori_loop(0, ME // 2 - 1, first_rows, 0)
    first_rows(ME // 2 - 1, 0)

    colf = jnp.where((jcol >= D) & (jcol < D + M), 1.0, 0.0)
    sub8 = lax.broadcasted_iota(jnp.int32, (SUB, LANES), 0)
    zero = jnp.zeros((ME, LANES), F32)

    def product(start, n):
        rows = pl.ds(mult(start), n)
        total = dot(Lr[rows, :], Xr[...])
        for j in PIECES:
            for i in PIECES[:len(PIECES) - j]:
                total = total + dot(L[rows, KM * i:KM * (i + 1)], X[j])
        return total

    def put_t(out, c):
        for h in HALVES:
            T[h, pl.ds(1 + ROWS * c, ROWS)] = out[:, lanes(h)].reshape(ROWS, ME, LANES)

    def v_copy(e):
        return rc(T.at[:, pl.ds(1 + (M - 1) * e, STRIP)], V.at[1 - e], v_s.at[e], v_r.at[1 - e], {"sx": sx - 1 + 2 * e})

    def step(m, carry):
        par = lax.rem(m, 2)

        def side(n, src, dst):
            return [rc(src[j], dst.at[par, 1 - j], hm_s.at[par, j, n], hm_r.at[par, 1 - j, n], (left, right)[j]) for j in HALVES]

        def go(pair):
            pl.when(has_left)(pair[0].start)
            pl.when(has_right)(pair[1].start)

        def cols(ref, lo, n):
            return [ref.at[:, pl.ds(lo, n), pl.ds(M * j, SUB)] for j in HALVES]

        mids = [side(n, cols(T, EDGE + ROWS * n, ROWS), HB.at[:, :, n]) for n in HALVES]
        edges = [side(2 + e, cols(TE, EDGE * e, EDGE), HE.at[:, :, e]) for e in (near, 1 - near)]
        ring = side(SIDE, (PK.at[0], PK.at[1]), HP)
        everything = mids + edges + [ring]
        v_near, v_far = v_copy(near), v_copy(1 - near)

        def edge(e, pair):
            for h in HALVES:
                TE[h, pl.ds((EDGE + 2) * e, STRIP)] = T[h, pl.ds((M + 1) * e, STRIP)] + V[e, h]
                TE[h, pl.ds(STRIP + 2 * e, 2)] = T[h, pl.ds(STRIP + 2 * EDGE * e, 2)]
            go(pair)

        first = m == 0
        c0, c3 = LAST * near, LAST * (1 - near)
        for h in HALVES:
            G1d[mine_y, h] = pqs[h][None]
        each(d1, "start")
        out = product((LAST * CHUNK + BT) * near, CHUNK + BT)
        put_t(out[BT:], c0)
        for h in HALVES:
            G1a[mine_y, h] = out[0:SUB, lanes(h)][None]
        each(a1, "start")
        pl.when(inner)(v_near.start)
        pl.when(jnp.logical_not(inner))(lambda: edge(near, edges[0]))
        put_t(product(BT + CHUNK, CHUNK), 1)
        go(mids[0])
        half_sum(G1d, G2d, d1, d2)
        put_t(product(BT + 2 * CHUNK, CHUNK), 2)
        go(mids[1])
        each(a1, "wait")
        each(a2, "start")

        pq = full_sum(G2d, d2)
        alpha = [jnp.where(first, -1.0, row(cst[0, h], 0) / row(pq[h], 0)) for h in HALVES]
        tot = [[zero, zero] for h in HALVES]

        def update(c, inside):
            for h in HALVES:
                for k in range(ROWS):
                    i = 1 + ROWS * c + k
                    rn = r[h, i] - alpha[h] * Q[h, i]
                    ln = l[h, i] - alpha[h] * T[h, i]
                    r[h, i] = rn
                    l[h, i] = ln
                    x[h, i] = x[h, i] + alpha[h] * p[h, i]
                    w = colf if inside else jnp.where((i >= OWN) & (i < OWN + M), 1.0, 0.0) * colf
                    tot[h][0] = tot[h][0] + rn * ln
                    tot[h][1] = tot[h][1] + w * (rn * rn)

        out = product(BT + (LAST * CHUNK + BT) * (1 - near), CHUNK)
        update(c0, False)
        update(1, True)
        update(2, True)
        put_t(out, c3)
        v_far.start()
        G2a[mine_x] = G1a[...][None]
        each(a2, "wait_send")
        update(c3, False)
        for h in HALVES:
            G1b[mine_y, h] = jnp.where(sub8 == 0, colsum(tot[h][0]), jnp.where(sub8 == 1, colsum(tot[h][1]), 0.0))[None]
        each(b1, "start")

        @pl.when(inner)
        def _():
            v_near.wait_send()
            rc(T.at[:, pl.ds(1, STRIP)], V.at[near], v_s.at[near], v_r.at[near], left).wait_recv()
            edge(near, edges[0])

        v_far.wait_send()
        rc(T.at[:, pl.ds(1, STRIP)], V.at[1 - near], v_s.at[near], v_r.at[1 - near], left).wait_recv()
        edge(1 - near, edges[1])
        for h in HALVES:
            for i in range(1, ME + 1):
                src, k = (TE, i) if i < EDGE else ((T, i) if i < M - 1 else (TE, i - 2 * ROWS))
                PK[0, h, i - 1:i] = src[h, k, SUB:SUB + 1]
                PK[1, h, i - 1:i] = src[h, k, M - 1:M]
        go(ring)

        each(a2, "wait_recv")
        cq = jnp.concatenate([G2a[:, :, h].reshape(LANES, LANES) for h in HALVES], axis=1)
        yq = dot_pieces(lambda at: Ccat[:, at:at + TILE], cq)
        rzc = []
        for h in HALVES:
            cr[h] = cr[h] - alpha[h] * cq[:, lanes(h)]
            wr[h] = wr[h] - alpha[h] * yq[:, lanes(h)]
            rzc.append(colsum(cr[h] * wr[h]))
        n = LOW // 2
        for part in HALVES:
            o = dot_pieces(lambda at: Ecat[ME * n * part:ME * n * (part + 1), at:at + TILE], yq)
            for h in HALVES:
                Ey[h, n * part:n * (part + 1)] = o[:, lanes(h)].reshape(n, ME, LANES)

        half_sum(G1b, G2b, b1, b2)
        got = full_sum(G2b, b2)
        beta = []
        for h in HALVES:
            rzn = row(got[h], 0) + rzc[h]
            rr = row(got[h], 1)
            beta.append(jnp.where(first, 0.0, rzn / row(cst[0, h], 0)))
            ff = jnp.where(first, jnp.sqrt(rr), row(cst[1, h], 0))
            cst[0, h] = wide(rzn)
            cst[1, h] = wide(ff)
            nrm_ref[:, lanes(h)] = jnp.where(sub8 == m - 1, jnp.sqrt(rr) / ff, nrm_ref[:, lanes(h)])

        for pair in everything:
            pl.when(has_right)(pair[0].wait_recv)
            pl.when(has_left)(pair[1].wait_recv)

        def renew(i, u):
            for h in HALVES:
                zn = z[h, i] - alpha[h] * (u[h] + Ey[h, i])
                z[h, i] = zn
                p[h, i] = zn + beta[h] * p[h, i]

        def sides(b, buf, n, h, k):
            return jnp.concatenate([b[0:SUB] + buf[par, 0, n, h, k], b[SUB:M], b[M:] + buf[par, 1, n, h, k]], axis=0)

        def mid_rows(k, c):
            for n in HALVES:
                i = EDGE + ROWS * n + k
                renew(i, [sides(T[h, i], HB, n, h, k) for h in HALVES])
            return c
        lax.fori_loop(0, ROWS, mid_rows, 0)

        def edge_rows(k, c):
            for n in HALVES:
                renew((M - 1) * n + k, [sides(TE[h, EDGE * n + k], HE, n, h, k) for h in HALVES])
            return c
        lax.fori_loop(0, EDGE, edge_rows, 0)
        for j in HALVES:
            renew(LOW - 2 + j, [HP[par, j, h] for h in HALVES])

        def apply_rows(g, car):
            sums = list(car)
            for h in HALVES:
                lring, rring = [p[h, LOW - 2 + j, pl.ds(mult(SUB * g, SUB), SUB), :] for j in HALVES]
                rows = []
                for k in range(SUB):
                    i = SUB * g + k
                    c = p[h, i + 1]
                    west = jnp.where(jcol == 0, row(lring, k), pltpu.roll(c, 1, 0))
                    east = jnp.where(jcol == ME - 1, row(rring, k), pltpu.roll(c, ME - 1, 0))
                    q = W5[SIDE, i] * c
                    for j, other in enumerate((p[h, i], p[h, i + 2], west, east)):
                        q = q - W5[j, i] * other
                    Q[h, i + 1] = q
                    sums[h] = sums[h] + jnp.where((i >= D) & (i < D + M), 1.0, 0.0) * colf * (c * q)
                    rows.append(q)
                    if len(rows) == 2:
                        put_x(rows, h, D * g + k // 2)
                        rows = []
            return tuple(sums)
        car = lax.fori_loop(0, ME // SUB - 1, apply_rows, (zero, zero))
        car = apply_rows(ME // SUB - 1, car)
        for h in HALVES:
            pqs[h] = wide(colsum(car[h]))

        for pair in everything:
            pl.when(has_left)(pair[0].wait_send)
            pl.when(has_right)(pair[1].wait_send)
        return carry

    lax.fori_loop(0, ITERS, step, 0)

    for h in HALVES:
        G1d[mine_y, h] = pqs[h][None]
    each(d1, "start")
    half_sum(G1d, G2d, d1, d2)
    pq = full_sum(G2d, d2)
    alpha = [row(cst[0, h], 0) / row(pq[h], 0) for h in HALVES]

    def finish(i, car):
        res = []
        for h in HALVES:
            rn = r[h, i] - alpha[h] * Q[h, i]
            res.append(car[h] + colf * (rn * rn))
            xn = x[h, i] + alpha[h] * p[h, i]
            T[h, i, 0:M] = pltpu.roll(jnp.concatenate([xn, xn[0:SUB]], axis=0), WIDE - D, 0)[0:M]
        return tuple(res)
    rr = lax.fori_loop(OWN, OWN + M, finish, (zero, zero))
    out_cp = [pltpu.make_async_copy(T.at[h, own, pl.ds(0, M)], x_hbm.at[:, :, pl.ds(LANES * h, LANES)], out_sem.at[h]) for h in HALVES]
    each(out_cp, "start")
    for h in HALVES:
        G1b[mine_y, h] = wide(colsum(rr[h]))[None]
    each(b1, "start")
    half_sum(G1b, G2b, b1, b2)
    got = full_sum(G2b, b2)
    for h in HALVES:
        nrm_ref[:, lanes(h)] = jnp.where(sub8 == ITERS - 1, jnp.sqrt(row(got[h], 0)) / row(cst[1, h], 0), nrm_ref[:, lanes(h)])
    each(out_cp, "wait")


def solution(mesh):
    def dma(*shape):
        return pltpu.SemaphoreType.DMA(shape)

    def vm(*shape, dtype=F32):
        return pltpu.VMEM(shape, dtype)

    field = vm(2, LOW, ME, LANES)
    strips = [vm(2, 2, 2, 2, n, SUB, LANES) for n in (ROWS, EDGE)]
    gathers = [vm(SIDE, 2, SUB, LANES), vm(SIDE, SIDE, 2, SUB, LANES)] + [vm(SIDE, 2, SUB, LANES)] * SIDE
    scratch = [
        vm(SIDE, M + 2 * OWN, WIDE, LANES), vm(NL, KM * len(PIECES), dtype=BF16), vm(NL, 2 * TILE, dtype=BF16),
        vm(SIDE, CHUNK, NE), vm(len(PIECES), KM, TILE, dtype=BF16), vm(2 * TILE, TILE, dtype=BF16),
        field, vm(2, 2 * EDGE, ME, LANES), field, field, field, field, field, field, field,
        vm(SIDE + 1, ME, ME, LANES), vm(LOW * ME, LANES * len(PIECES), dtype=BF16), vm(2, ME, LANES),
        vm(2, 2, STRIP, ME, LANES), *strips, vm(2, 2, 2, ME, LANES), vm(2, 2, ME, LANES), *gathers,
        vm(LANES, LANES * len(PIECES), dtype=BF16), vm(2, LANES, LANES), vm(2, LANES, LANES), vm(2, 2, SUB, LANES),
        vm(2, SUB, LANES), dma(SIDE), dma(SIDE), *[dma(2)] * 6, *[dma(2, 2, SIDE + 1)] * 2, *[dma(LAST)] * 12, dma(2),
    ]
    any_spec = pl.BlockSpec(memory_space=pl.ANY)
    vmem_spec = pl.BlockSpec(memory_space=pltpu.VMEM)

    def body(forcing, kappa, local_inv, coarse_basis, coarse_counts, coarse_inv):
        index = lax.axis_index("sx") * SIDE + lax.axis_index("sy")
        basis = coarse_basis[0]
        mine = jnp.arange(LANES) // KMAX == index
        spread = jnp.where(mine[None, :], jnp.tile(basis, (1, LANES // KMAX)), 0.0)
        aux = jnp.stack([spread.reshape(M, M, LANES), jnp.broadcast_to(kappa[:, :, None], (M, M, LANES))])
        bt = jnp.pad(basis.T.reshape(KMAX, M, M), ((0, BT - KMAX), (D, D), (D, D))).reshape(BT, NE)
        cnt = jnp.broadcast_to(jnp.where(mine, coarse_counts.astype(F32), 0.0)[None, :], (SUB, LANES))
        return pl.pallas_call(
            solve_kernel,
            out_shape=(jax.ShapeDtypeStruct((M, M, 2 * LANES), F32), jax.ShapeDtypeStruct((ITERS, 2 * LANES), F32)),
            in_specs=[any_spec] * len(PIECES) + [vmem_spec] * len(PIECES),
            out_specs=(any_spec, vmem_spec),
            scratch_shapes=scratch,
            compiler_params=pltpu.CompilerParams(collective_id=0, has_side_effects=True, vmem_limit_bytes=67043328),
        )(forcing, aux, local_inv[0], bt, coarse_inv, cnt)

    cell_spec = P(("batch", "sx"), "sy", None)
    sub_spec = P(("batch", "sx", "sy"), None, None)
    return jax.shard_map(body, mesh=mesh, in_specs=(cell_spec, P(("batch", "sx"), "sy"), sub_spec, sub_spec, P(("batch", "sx", "sy")), P("batch", None)), out_specs=(cell_spec, P("batch", None)), check_vma=False)
```

time: 1350 us -> 268 us (0.20); the launches traced: 1330 us -> 267 us
  blocking collectives: 794 us -> 0 us
  Pallas kernels: 0 us -> 255 us
  starting transfers between devices: 180 us -> 0 us
  matrix products: 118 us -> 0 us
  waiting for transfers between devices: 103 us -> 0 us
  other arithmetic: 85.5 us -> 1.1 us
  local copies, waits for them, and re-layouts: 48.7 us -> 9.62 us
    psum x16 -> x0, blocking collectives: 523 us -> none  [the longest x9 288 us: global_dot(): return lax.psum(jnp.sum(first * second, axis=(0, 1)), grid_axes)]
    all_gather x8 -> x0, blocking collectives: 257 us -> none  [schwarz(): gathered = lax.all_gather(restrict, grid_axes, tiled=True)]
    pallas_call x0 -> x1, Pallas kernels: none -> 255 us  [body(): pl.pallas_call(solve_kernel, out_shape=(jax.ShapeDtypeStruct((M, M, 2 * L...]
    ppermute x100 -> x0, starting transfers between devices: 180 us -> none  [the longest x8 36.4 us: schwarz(): back_right = lax.ppermute(local[:, size + over:], 'sy', to_right)]
    dot_general x34 -> x0, matrix products: 118 us -> none  [the longest x26 112 us: matmul(): jnp.dot(first, second, precision=highest, preferred_element_type=jnp.floa...]
    ppermute x100 -> x0, waiting for transfers between devices: 103 us -> none  [the longest x8 36 us: schwarz(): from_bottom = lax.ppermute(resid[:over], 'sx', to_above)]
    reduce_sum x16 -> x0, other arithmetic: 33.8 us -> none  [the longest x9 19.7 us: global_dot(): return lax.psum(jnp.sum(first * second, axis=(0, 1)), grid_axes)]
    select_n x6 -> x2, other arithmetic: 21.3 us -> 0.04 us  [the longest x1 0.04 us: body(): spread = jnp.where(mine[None, :], jnp.tile(basis, (1, LANES // KMAX)), 0.0)]
  transfers between devices with their start and end apart: 100 -> 0, of which waited for: 42 -> 0; matrix products, arithmetic and copies ran while one was open for 6% -> 0% of each run, Pallas kernels for 0% -> 0%
where the time goes in v1:
time: 268 us; the launch traced here: 267 us
  Pallas kernels  255 us (95%)
  local copies, waits for them, and re-layouts  9.62 us (4%)
    pallas_call x1, Pallas kernels, body(): pl.pallas_call(solve_kernel, out_shape=(jax.ShapeDtypeStruct((M, M, 2 * L...  255 us

profile of v1, /device:TPU:0, one launch (start us, length us, event | category | flops | bytes accessed | tf_op | source)
XLA Modules:
  0.0 267.4 jit_solution(3984465932938399666)
XLA Ops:
  0.6 0.8 tile.11
  1.5 0.7 tile.12
  2.1 1.3 copy.9
  3.5 0.9 stack_broadcast_in_dim.2
  4.4 1.0 pad_maximum_fusion.aux_hbm
  6.1 0.6 broadcast_in_dim.39.cnt_ref
  6.7 0.8 reshape.48
  7.5 0.1 pad.4
  7.7 0.8 reshape.49.bt_ref
  8.4 255.4 %shard_map.77 = (f32[32,32,256]{2,1,0:T(8,128)}, f32[8,256]{1,0:T(8,128)}) custom-call(f32[32,32,256]{2,1,0:T(8,128)} %f_hbm.1, f32[2,32,32,128]{3,2,1,0:T(8,128)} %pad_maximum_fusion.aux_hbm, f32[1600,1600]{1,0:T(8,128)} %bitcast.7, f32[16,1600]{1,0:T(8,128)} %reshape.49.bt_ref, f32[64,64]{1,0:T(8,128)} %cinv_ref.1, f32[8,128]{1,0:T(8,128)} %broadcast_in_dim.39.cnt_ref), custom_call_target="tpu_custom_call" | custom-call | tf_op jit(solution)/shard_map/pallas_call | solution.py:556
  263.8 2.3 copy.13
  266.1 1.3 copy.14
  (3 shorter events, 0.1 us)

commit v2 on v1

--- a/solution.py
+++ b/solution.py
@@ -18,6 +18,7 @@
 REM = NE - KM
 ROWS = 10
 CHUNK = ROWS * ME
+NA = 208
 BT = 16
 NL = NE + 2 * BT
 KMAX = 8
@@ -304,16 +305,27 @@
     zero = jnp.zeros((ME, LANES), F32)
 
     def product(start, n):
-        rows = pl.ds(mult(start), n)
-        total = dot(Lr[rows, :], Xr[...])
-        for j in PIECES:
-            for i in PIECES[:len(PIECES) - j]:
-                total = total + dot(L[rows, KM * i:KM * (i + 1)], X[j])
-        return total
-
-    def put_t(out, c):
-        for h in HALVES:
-            T[h, pl.ds(1 + ROWS * c, ROWS)] = out[:, lanes(h)].reshape(ROWS, ME, LANES)
+        first = NA
+        outs = []
+        for at, size in ((0, first), (first, n - first)):
+            rows = pl.ds(mult(start + at), size)
+            total = dot(Lr[rows, :], Xr[...])
+            for j in PIECES:
+                for i in PIECES[:len(PIECES) - j]:
+                    total = total + dot(L[rows, KM * i:KM * (i + 1)], X[j])
+            outs.append(total)
+        return outs
+
+    def put_t(outs, c):
+        at = 0
+        for v in outs:
+            while v.shape[0]:
+                top, off = 1 + ROWS * c + at // ME, at % ME
+                n = min(ME - off, v.shape[0]) if off or v.shape[0] < ME else v.shape[0] // ME * ME
+                whole = max(n // ME, 1)
+                for h in HALVES:
+                    T[h, pl.ds(top, whole), off:off + n // whole] = v[0:n, lanes(h)].reshape(whole, n // whole, LANES)
+                v, at = v[n:], at + n
 
     def v_copy(e):
         return rc(T.at[:, pl.ds(1 + (M - 1) * e, STRIP)], V.at[1 - e], v_s.at[e], v_r.at[1 - e], {"sx": sx - 1 + 2 * e})
@@ -349,9 +361,9 @@
             G1d[mine_y, h] = pqs[h][None]
         each(d1, "start")
         out = product((LAST * CHUNK + BT) * near, CHUNK + BT)
-        put_t(out[BT:], c0)
-        for h in HALVES:
-            G1a[mine_y, h] = out[0:SUB, lanes(h)][None]
+        put_t([out[0][BT:], out[1]], c0)
+        for h in HALVES:
+            G1a[mine_y, h] = out[0][0:SUB, lanes(h)][None]
         each(a1, "start")
         pl.when(inner)(v_near.start)
         pl.when(jnp.logical_not(inner))(lambda: edge(near, edges[0]))

time: 268 us -> 224 us (0.84)
  Pallas kernels: 255 us -> 211 us
    pallas_call x1, Pallas kernels: 255 us -> 211 us  [body(): pl.pallas_call(solve_kernel, out_shape=(jax.ShapeDtypeStruct((M, M, 2 * L...]
where the time goes in v2:
time: 224 us
  Pallas kernels  211 us (94%)
  local copies, waits for them, and re-layouts  9.62 us (4%)
    pallas_call x1, Pallas kernels, body(): pl.pallas_call(solve_kernel, out_shape=(jax.ShapeDtypeStruct((M, M, 2 * L...  211 us

profile of v2, /device:TPU:0, one launch (start us, length us, event | category | flops | bytes accessed | tf_op | source)
XLA Modules:
  0.0 223.5 jit_solution(3745343716869260025)
XLA Ops:
  0.6 0.8 tile.11
  1.5 0.7 tile.12
  2.1 1.3 copy.9
  3.5 0.9 stack_broadcast_in_dim.2
  4.4 1.0 pad_maximum_fusion.aux_hbm
  6.1 0.6 broadcast_in_dim.39.cnt_ref
  6.7 0.8 reshape.48
  7.5 0.1 pad.4
  7.7 0.8 reshape.49.bt_ref
  8.4 211.5 %shard_map.77 = (f32[32,32,256]{2,1,0:T(8,128)}, f32[8,256]{1,0:T(8,128)}) custom-call(f32[32,32,256]{2,1,0:T(8,128)} %f_hbm.1, f32[2,32,32,128]{3,2,1,0:T(8,128)} %pad_maximum_fusion.aux_hbm, f32[1600,1600]{1,0:T(8,128)} %bitcast.7, f32[16,1600]{1,0:T(8,128)} %reshape.49.bt_ref, f32[64,64]{1,0:T(8,128)} %cinv_ref.1, f32[8,128]{1,0:T(8,128)} %broadcast_in_dim.39.cnt_ref), custom_call_target="tpu_custom_call" | custom-call | tf_op jit(solution)/shard_map/pallas_call | solution.py:568
  219.9 2.3 %copy.13 = f32[32,32,256]{2,1,0:T(8,128)} copy(f32[32,32,256]{2,1,0:T(8,128)} %get-tuple-element.4) | data formatting | bytes 2097152
  222.3 1.3 copy.14
  (3 shorter events, 0.1 us)

commit v3 on v2

--- a/solution.py
+++ b/solution.py
@@ -18,6 +18,7 @@
 REM = NE - KM
 ROWS = 10
 CHUNK = ROWS * ME
+NP = NE + REM
 NA = 208
 BT = 16
 NL = NE + 2 * BT
@@ -76,10 +77,10 @@
     return hi, mid, low
 
 
-def solve_kernel(f_hbm, aux_hbm, inv_hbm, bt_ref, cinv_ref, cnt_ref, x_hbm, nrm_ref,
-                 S48, L, Lr, stage, X, Xr, T, TE, z, p, r, l, x, Q, Ey, W5, Ecat, RE,
+def solve_kernel(f_hbm, inv_hbm, own_ref, cinv_ref, cnt_ref, x_hbm, nrm_ref,
+                 S48, L, Lr, stage, X, Xr, T, TE, z, p, r, l, x, Q, Ey, W5, Ecat, RE, KB, FL,
                V, HB, HE, HP, PK, G1a, G2a, G1b, G2b, G1d, G2d, Ccat, cr, wr, cst, pqs,
-               ld_sem, own_sem, h0_s, h0_r, v0_s, v0_r, v_s, v_r, hm_s, hm_r,
+               ld_sem, own_sem, h0_s, h0_r, v0_s, v0_r, h1_s, h1_r, v1_s, v1_r, v_s, v_r, hm_s, hm_r,
                a1_s, a1_r, a2_s, a2_r, b1_s, b1_r, b2_s, b2_r, d1_s, d1_r, d2_s, d2_r, out_sem):
     sx = lax.axis_index("sx")
     sy = lax.axis_index("sy")
@@ -95,13 +96,12 @@
     own = pl.ds(OWN, M)
     inv_cp = [pltpu.make_async_copy(inv_hbm.at[pl.ds(CHUNK * c, CHUNK)], stage.at[c], ld_sem.at[c]) for c in range(SIDE)]
     own_cp = [pltpu.make_async_copy(f_hbm.at[:, :, pl.ds(LANES * h, LANES)], S48.at[h, own, pl.ds(SUB, M)], own_sem.at[h]) for h in HALVES]
-    own_cp += [pltpu.make_async_copy(aux_hbm.at[h], S48.at[2 + h, own, pl.ds(SUB, M)], own_sem.at[2 + h]) for h in HALVES]
     each(own_cp, "start")
     each(inv_cp, "start")
-    zrow = jnp.zeros((SIDE, OWN, WIDE, LANES), F32)
+    zrow = jnp.zeros((len(PIECES), OWN, WIDE, LANES), F32)
     S48[:, 0:OWN] = zrow
     S48[:, OWN + M:] = zrow
-    zcol = jnp.zeros((SIDE, M, SUB, LANES), F32)
+    zcol = jnp.zeros((len(PIECES), M, SUB, LANES), F32)
     S48[:, OWN:OWN + M, 0:SUB] = zcol
     S48[:, OWN:OWN + M, ME:] = zcol
     for b in (V, HB, HE, HP):
@@ -139,14 +139,65 @@
     G1b[mine_y] = jnp.broadcast_to(cnt_ref[...], (1, 2, SUB, LANES))
     each(b1, "start")
 
+    def halos(slabs, hs, hr, vs, vr):
+        h = [rc(S48.at[slabs, own, pl.ds(SUB, SUB)], S48.at[slabs, own, pl.ds(ME, SUB)], hs.at[0], hr.at[0], left),
+             rc(S48.at[slabs, own, pl.ds(M, SUB)], S48.at[slabs, own, pl.ds(0, SUB)], hs.at[1], hr.at[1], right)]
+        v = [rc(S48.at[slabs, pl.ds(OWN, OWN)], S48.at[slabs, pl.ds(OWN + M, OWN)], vs.at[0], vr.at[1], {"sx": sx - 1}),
+             rc(S48.at[slabs, pl.ds(M, OWN)], S48.at[slabs, pl.ds(0, OWN)], vs.at[1], vr.at[0], {"sx": sx + 1})]
+        v_in = [rc(S48.at[slabs, pl.ds(0, OWN)], S48.at[slabs, pl.ds(0, OWN)], vs.at[e], vr.at[e], left) for e in HALVES]
+        return h, v, v_in
+    f_h, f_v, f_in = halos(pl.ds(0, 2), h0_s, h0_r, v0_s, v0_r)
+    k_h, k_v, k_in = halos(pl.ds(2, 1), h1_s, h1_r, v1_s, v1_r)
+
+    def go(pair):
+        pl.when(has_left)(pair[0].start)
+        pl.when(has_right)(pair[1].start)
+
+    def come(pair):
+        pl.when(has_right)(pair[0].wait_recv)
+        pl.when(has_left)(pair[1].wait_recv)
+
+    def gone(pair):
+        pl.when(has_left)(pair[0].wait_send)
+        pl.when(has_right)(pair[1].wait_send)
+
+    def up_down(pair, what):
+        for e in HALVES:
+            pl.when(has[e])(getattr(pair[e], what))
     each(own_cp, "wait")
-    h0l = rc(S48.at[:, own, pl.ds(SUB, SUB)], S48.at[:, own, pl.ds(ME, SUB)], h0_s.at[0], h0_r.at[0], left)
-    h0r = rc(S48.at[:, own, pl.ds(M, SUB)], S48.at[:, own, pl.ds(0, SUB)], h0_s.at[1], h0_r.at[1], right)
-    v0 = [rc(S48.at[:, pl.ds(OWN, OWN)], S48.at[:, pl.ds(OWN + M, OWN)], v0_s.at[0], v0_r.at[1], {"sx": sx - 1}),
-          rc(S48.at[:, pl.ds(M, OWN)], S48.at[:, pl.ds(0, OWN)], v0_s.at[1], v0_r.at[0], {"sx": sx + 1})]
-    v0_in = [rc(S48.at[:, pl.ds(0, OWN)], S48.at[:, pl.ds(0, OWN)], v0_s.at[e], v0_r.at[e], left) for e in HALVES]
-    pl.when(has_left)(h0l.start)
-    pl.when(has_right)(h0r.start)
+    go(f_h)
+
+    slot = mult(KMAX * (sx * SIDE + sy), KMAX)
+    FL[...] = jnp.zeros(FL.shape, F32)
+    FL[pl.ds(slot, KMAX), 0:M * M] = own_ref[...]
+    for k in range(SUB):
+        S48[2, OWN + D * k:OWN + D * (k + 1), SUB:ME] = FL[:, lanes(k)].T.reshape(D, M, LANES)
+    go(k_h)
+
+    def shifted(v, k=D):
+        return pltpu.roll(v, WIDE - k, 0)[0:ME]
+    lane_of = lax.broadcasted_iota(jnp.int32, (WIDE, LANES), 1)
+    last_slot = lane_of % KMAX == KMAX - 1
+
+    def basis_of(v):
+        return jnp.where(last_slot[0:ME], 0.0, v)
+
+    def own_rows(i, c):
+        mine = S48[2, i + 1, SUB:ME]
+        mine = jnp.concatenate([mine, jnp.zeros((BT, LANES), F32)], axis=0)
+        W5[0, i] = basis_of(pltpu.roll(mine, D, 0)[0:ME])
+        return c
+    for i in list(range(D)) + list(range(D + M, ME)):
+        W5[0, i] = jnp.zeros((ME, LANES), F32)
+    lax.fori_loop(D, D + M, own_rows, 0)
+    flat = W5[0].reshape(NE, LANES)
+    for k in range(NP // LANES):
+        blk = flat[LANES * k:LANES * (k + 1)]
+        if blk.shape[0] < LANES:
+            blk = jnp.concatenate([blk, jnp.zeros_like(blk)], axis=0)
+        FL[:, lanes(k)] = blk.T
+    restrict = FL[pl.ds(slot, KMAX), 0:NE]
+    restrict = jnp.concatenate([restrict, jnp.zeros_like(restrict)], axis=0)
 
     for b in (p, z, r, l, x, T):
         def zero(i, c, b=b):
@@ -170,7 +221,7 @@
         Lr[rows, lanes(LAST)] = jnp.zeros(twice.shape, BF16)
 
     for at in (0, LAST * CHUNK + BT):
-        put_l(bt_ref[...], pl.ds(at, BT))
+        put_l(restrict, pl.ds(at, BT))
     half_sum(G1b, G2b, b1, b2)
 
     def split_inv(c):
@@ -183,12 +234,9 @@
 
     split_inv(0)
     split_inv(1)
-    pl.when(has_left)(h0l.wait_send)
-    pl.when(has_right)(h0r.wait_send)
-    pl.when(has_right)(h0l.wait_recv)
-    pl.when(has_left)(h0r.wait_recv)
-    for e in HALVES:
-        pl.when(has[e])(v0[e].start)
+    come(f_h)
+    gone(f_h)
+    up_down(f_v, "start")
     split_inv(2)
     split_inv(LAST)
 
@@ -231,28 +279,31 @@
             ref[rows, lanes(k)] = piece
     put_middle(Ccat, pl.ds(0, LANES), spread)
 
-    for e in HALVES:
-        pl.when(has[e])(v0[e].wait_send)
-        pl.when(has[e])(v0_in[e].wait_recv)
+    come(k_h)
+    gone(k_h)
+    up_down(k_v, "start")
+    up_down(f_v, "wait_send")
+    up_down(f_in, "wait_recv")
 
     jcol = lax.broadcasted_iota(jnp.int32, (ME, LANES), 0)
     gj = sy * M + jcol - D
     in_col = (gj >= 0) & (gj < GRID)
 
-    def shifted(v, k=D):
-        return pltpu.roll(v, WIDE - k, 0)[0:ME]
+    def kappa_rows(i, c):
+        KB[i] = jnp.broadcast_to(jnp.sum(jnp.where(last_slot, S48[2, i], 0.0), axis=1, keepdims=True), (WIDE, LANES))
+        return c
 
     def weights(i, c):
         gi = sx * M + i - D
         ok = in_col & (gi >= 0) & (gi < GRID)
-        here = S48[LAST, i + 1]
+        here = KB[i + 1]
         kc = shifted(here)
 
         def pair(other, inside):
             both = ok & inside
             w = jnp.where(both, 2.0 * kc * other / jnp.where(both, kc + other, 1.0), 0.0)
             return w, jnp.where(ok & jnp.logical_not(inside), kc, w)
-        edges = (pair(shifted(S48[LAST, i]), ok & (gi > 0)), pair(shifted(S48[LAST, i + 2]), ok & (gi < GRID - 1)),
+        edges = (pair(shifted(KB[i]), ok & (gi > 0)), pair(shifted(KB[i + 2]), ok & (gi < GRID - 1)),
                  pair(shifted(here, D - 1), gj > 0), pair(shifted(here, D + 1), gj < GRID - 1))
         total = 0.0
         for k, (w, d) in enumerate(edges):
@@ -260,22 +311,25 @@
             total = total + d
         W5[SIDE, i] = total
         return c
-    lax.fori_loop(0, ME, weights, 0)
-
-    for i in range(ME):
-        RE[0, i:i + 1] = S48[2, i + 1, D - 1:D]
-        RE[1, i:i + 1] = S48[2, i + 1, LOW:LOW + 1]
 
     def pair_of(two, k):
         return jnp.concatenate(two, axis=0), pl.ds(mult(2 * ME * k), 2 * ME)
 
     def basis_rows(k, c):
-        v, rows = pair_of([shifted(S48[2, 2 * k]), shifted(S48[2, 2 * k + 1])], k)
+        v, rows = pair_of([basis_of(shifted(S48[2, 2 * k + j])) for j in HALVES], k)
         put_middle(Ecat, rows, v)
         return c
-    lax.fori_loop(0, LOW // 2 - 1, basis_rows, 0)
-    v, rows = pair_of([RE[0], RE[1]], LOW // 2 - 1)
-    put_middle(Ecat, rows, v)
+    def geometry():
+        up_down(k_v, "wait_send")
+        up_down(k_in, "wait_recv")
+        lax.fori_loop(0, M + 2 * OWN, kappa_rows, 0)
+        lax.fori_loop(0, ME, weights, 0)
+        for i in range(ME):
+            RE[0, i:i + 1] = S48[2, i + 1, D - 1:D]
+            RE[1, i:i + 1] = S48[2, i + 1, LOW:LOW + 1]
+        lax.fori_loop(0, LOW // 2 - 1, basis_rows, 0)
+        v, rows = pair_of([basis_of(RE[j]) for j in HALVES], LOW // 2 - 1)
+        put_middle(Ecat, rows, v)
 
     def put_x(two, h, k):
         v, rows = pair_of(two, k)
@@ -336,10 +390,6 @@
         def side(n, src, dst):
             return [rc(src[j], dst.at[par, 1 - j], hm_s.at[par, j, n], hm_r.at[par, 1 - j, n], (left, right)[j]) for j in HALVES]
 
-        def go(pair):
-            pl.when(has_left)(pair[0].start)
-            pl.when(has_right)(pair[1].start)
-
         def cols(ref, lo, n):
             return [ref.at[:, pl.ds(lo, n), pl.ds(M * j, SUB)] for j in HALVES]
 
@@ -421,6 +471,7 @@
                 PK[1, h, i - 1:i] = src[h, k, M - 1:M]
         go(ring)
 
+        pl.when(first)(geometry)
         each(a2, "wait_recv")
         cq = jnp.concatenate([G2a[:, :, h].reshape(LANES, LANES) for h in HALVES], axis=1)
         yq = dot_pieces(lambda at: Ccat[:, at:at + TILE], cq)
@@ -448,8 +499,7 @@
             nrm_ref[:, lanes(h)] = jnp.where(sub8 == m - 1, jnp.sqrt(rr) / ff, nrm_ref[:, lanes(h)])
 
         for pair in everything:
-            pl.when(has_right)(pair[0].wait_recv)
-            pl.when(has_left)(pair[1].wait_recv)
+            come(pair)
 
         def renew(i, u):
             for h in HALVES:
@@ -477,23 +527,25 @@
 
         def apply_rows(g, car):
             sums = list(car)
-            for h in HALVES:
-                lring, rring = [p[h, LOW - 2 + j, pl.ds(mult(SUB * g, SUB), SUB), :] for j in HALVES]
-                rows = []
-                for k in range(SUB):
-                    i = SUB * g + k
+            rings = [[p[h, LOW - 2 + j, pl.ds(mult(SUB * g, SUB), SUB), :] for j in HALVES] for h in HALVES]
+            rows = [[], []]
+            for k in range(SUB):
+                i = SUB * g + k
+                w = [W5[j, i] for j in range(SIDE + 1)]
+                own_f = jnp.where((i >= D) & (i < D + M), 1.0, 0.0) * colf
+                for h in HALVES:
                     c = p[h, i + 1]
-                    west = jnp.where(jcol == 0, row(lring, k), pltpu.roll(c, 1, 0))
-                    east = jnp.where(jcol == ME - 1, row(rring, k), pltpu.roll(c, ME - 1, 0))
-                    q = W5[SIDE, i] * c
+                    west = jnp.where(jcol == 0, row(rings[h][0], k), pltpu.roll(c, 1, 0))
+                    east = jnp.where(jcol == ME - 1, row(rings[h][1], k), pltpu.roll(c, ME - 1, 0))
+                    q = w[SIDE] * c
                     for j, other in enumerate((p[h, i], p[h, i + 2], west, east)):
-                        q = q - W5[j, i] * other
+                        q = q - w[j] * other
                     Q[h, i + 1] = q
-                    sums[h] = sums[h] + jnp.where((i >= D) & (i < D + M), 1.0, 0.0) * colf * (c * q)
-                    rows.append(q)
-                    if len(rows) == 2:
-                        put_x(rows, h, D * g + k // 2)
-                        rows = []
+                    sums[h] = sums[h] + own_f * (c * q)
+                    rows[h].append(q)
+                    if len(rows[h]) == 2:
+                        put_x(rows[h], h, D * g + k // 2)
+                        rows[h] = []
             return tuple(sums)
         car = lax.fori_loop(0, ME // SUB - 1, apply_rows, (zero, zero))
         car = apply_rows(ME // SUB - 1, car)
@@ -501,8 +553,7 @@
             pqs[h] = wide(colsum(car[h]))
 
         for pair in everything:
-            pl.when(has_left)(pair[0].wait_send)
-            pl.when(has_right)(pair[1].wait_send)
+            gone(pair)
         return carry
 
     lax.fori_loop(0, ITERS, step, 0)
@@ -546,33 +597,30 @@
     strips = [vm(2, 2, 2, 2, n, SUB, LANES) for n in (ROWS, EDGE)]
     gathers = [vm(SIDE, 2, SUB, LANES), vm(SIDE, SIDE, 2, SUB, LANES)] + [vm(SIDE, 2, SUB, LANES)] * SIDE
     scratch = [
-        vm(SIDE, M + 2 * OWN, WIDE, LANES), vm(NL, KM * len(PIECES), dtype=BF16), vm(NL, 2 * TILE, dtype=BF16),
+        vm(len(PIECES), M + 2 * OWN, WIDE, LANES), vm(NL, KM * len(PIECES), dtype=BF16), vm(NL, 2 * TILE, dtype=BF16),
         vm(SIDE, CHUNK, NE), vm(len(PIECES), KM, TILE, dtype=BF16), vm(2 * TILE, TILE, dtype=BF16),
         field, vm(2, 2 * EDGE, ME, LANES), field, field, field, field, field, field, field,
-        vm(SIDE + 1, ME, ME, LANES), vm(LOW * ME, LANES * len(PIECES), dtype=BF16), vm(2, ME, LANES),
+        vm(SIDE + 1, ME, ME, LANES), vm(LOW * ME, LANES * len(PIECES), dtype=BF16), vm(2, ME, LANES), vm(M + 2 * OWN, WIDE, LANES), vm(LANES, NP),
         vm(2, 2, STRIP, ME, LANES), *strips, vm(2, 2, 2, ME, LANES), vm(2, 2, ME, LANES), *gathers,
         vm(LANES, LANES * len(PIECES), dtype=BF16), vm(2, LANES, LANES), vm(2, LANES, LANES), vm(2, 2, SUB, LANES),
-        vm(2, SUB, LANES), dma(SIDE), dma(SIDE), *[dma(2)] * 6, *[dma(2, 2, SIDE + 1)] * 2, *[dma(LAST)] * 12, dma(2),
+        vm(2, SUB, LANES), dma(SIDE), dma(2), *[dma(2)] * 10, *[dma(2, 2, SIDE + 1)] * 2, *[dma(LAST)] * 12, dma(2),
     ]
     any_spec = pl.BlockSpec(memory_space=pl.ANY)
     vmem_spec = pl.BlockSpec(memory_space=pltpu.VMEM)
 
     def body(forcing, kappa, local_inv, coarse_basis, coarse_counts, coarse_inv):
         index = lax.axis_index("sx") * SIDE + lax.axis_index("sy")
-        basis = coarse_basis[0]
+        own = jnp.concatenate([coarse_basis[0].T[:KMAX - 1], kappa.reshape(1, M * M)], axis=0)
         mine = jnp.arange(LANES) // KMAX == index
-        spread = jnp.where(mine[None, :], jnp.tile(basis, (1, LANES // KMAX)), 0.0)
-        aux = jnp.stack([spread.reshape(M, M, LANES), jnp.broadcast_to(kappa[:, :, None], (M, M, LANES))])
-        bt = jnp.pad(basis.T.reshape(KMAX, M, M), ((0, BT - KMAX), (D, D), (D, D))).reshape(BT, NE)
         cnt = jnp.broadcast_to(jnp.where(mine, coarse_counts.astype(F32), 0.0)[None, :], (SUB, LANES))
         return pl.pallas_call(
             solve_kernel,
             out_shape=(jax.ShapeDtypeStruct((M, M, 2 * LANES), F32), jax.ShapeDtypeStruct((ITERS, 2 * LANES), F32)),
-            in_specs=[any_spec] * len(PIECES) + [vmem_spec] * len(PIECES),
+            in_specs=[any_spec] * 2 + [vmem_spec] * len(PIECES),
             out_specs=(any_spec, vmem_spec),
             scratch_shapes=scratch,
             compiler_params=pltpu.CompilerParams(collective_id=0, has_side_effects=True, vmem_limit_bytes=67043328),
-        )(forcing, aux, local_inv[0], bt, coarse_inv, cnt)
+        )(forcing, local_inv[0], own, coarse_inv, cnt)
 
     cell_spec = P(("batch", "sx"), "sy", None)
     sub_spec = P(("batch", "sx", "sy"), None, None)

time: 224 us -> 213 us (0.951)
  Pallas kernels: 211 us -> 205 us
  local copies, waits for them, and re-layouts: 9.62 us -> 4.99 us
    pallas_call x1, Pallas kernels: 211 us -> 205 us  [body(): pl.pallas_call(solve_kernel, out_shape=(jax.ShapeDtypeStruct((M, M, 2 * L...]
    another operation x4 -> x0, local copies, waits for them, and re-layouts: 3.67 us -> none  [the longest x3 2.76 us: body(): spread = jnp.where(mine[None, :], jnp.tile(basis, (1, LANES // KMAX)), 0.0)]
where the time goes in v3:
time: 213 us
  Pallas kernels  205 us (96%)
  local copies, waits for them, and re-layouts  4.99 us (2%)
    pallas_call x1, Pallas kernels, body(): pl.pallas_call(solve_kernel, out_shape=(jax.ShapeDtypeStruct((M, M, 2 * L...  205 us

profile of v3, /device:TPU:0, one launch (start us, length us, event | category | flops | bytes accessed | tf_op | source)
XLA Modules:
  0.0 213.0 jit_solution(17766603265406866574)
XLA Ops:
  1.3 0.6 broadcast_in_dim.23.cnt_ref
  1.9 0.8 reshape.22
  2.7 1.4 pad_maximum_fusion.own_ref
  4.1 205.3 %shard_map.77 = (f32[32,32,256]{2,1,0:T(8,128)}, f32[8,256]{1,0:T(8,128)}) custom-call(f32[32,32,256]{2,1,0:T(8,128)} %f_hbm.1, f32[1600,1600]{1,0:T(8,128)} %bitcast.6, f32[8,1024]{1,0:T(8,128)} %pad_maximum_fusion.own_ref, f32[64,64]{1,0:T(8,128)} %cinv_ref.1, f32[8,128]{1,0:T(8,128)} %broadcast_in_dim.23.cnt_ref), custom_call_target="tpu_custom_call" | custom-call | tf_op jit(solution)/shard_map/pallas_call | solution.py:616
  209.4 2.3 %copy.11 = f32[32,32,256]{2,1,0:T(8,128)} copy(f32[32,32,256]{2,1,0:T(8,128)} %get-tuple-element.4) | data formatting | bytes 2097152
  211.7 1.3 copy.12
  (1 shorter events, 0.0 us)

commit v4 on v3

--- a/solution.py
+++ b/solution.py
@@ -79,9 +79,9 @@
 
 def solve_kernel(f_hbm, inv_hbm, own_ref, cinv_ref, cnt_ref, x_hbm, nrm_ref,
                  S48, L, Lr, stage, X, Xr, T, TE, z, p, r, l, x, Q, Ey, W5, Ecat, RE, KB, FL,
-               V, HB, HE, HP, PK, G1a, G2a, G1b, G2b, G1d, G2d, Ccat, cr, wr, cst, pqs,
+               V, HB, HE, HP, PK, G1a, G2a, Gb, Gd, Ccat, cr, wr, cst, pqs,
                ld_sem, own_sem, h0_s, h0_r, v0_s, v0_r, h1_s, h1_r, v1_s, v1_r, v_s, v_r, hm_s, hm_r,
-               a1_s, a1_r, a2_s, a2_r, b1_s, b1_r, b2_s, b2_r, d1_s, d1_r, d2_s, d2_r, out_sem):
+               a1_s, a1_r, a2_s, a2_r, b_s, b_r, d_s, d_r, out_sem):
     sx = lax.axis_index("sx")
     sy = lax.axis_index("sy")
     left, right = {"sy": sy - 1}, {"sy": sy + 1}
@@ -108,36 +108,35 @@
         b[...] = jnp.zeros(b.shape, F32)
 
     bar = pltpu.get_barrier_semaphore()
-    for d in FAR:
-        pl.semaphore_signal(bar, inc=1, device_id={"sx": lax.rem(sx + d, SIDE)}, device_id_type=MESH)
-        pl.semaphore_signal(bar, inc=1, device_id={"sy": lax.rem(sy + d, SIDE)}, device_id_type=MESH)
-    pl.semaphore_wait(bar, 2 * LAST)
+    peers = [{"sx": lax.rem(sx + k // SIDE, SIDE), "sy": lax.rem(sy + k % SIDE, SIDE)} for k in range(1, SIDE * SIDE)]
+    for peer in peers:
+        pl.semaphore_signal(bar, inc=1, device_id=peer, device_id_type=MESH)
+    pl.semaphore_wait(bar, len(peers))
 
     def first_copies(G1, s, q):
         return [rc(G1.at[sy], G1.at[sy], s.at[d - 1], q.at[d - 1], {"sy": lax.rem(sy + d, SIDE)}) for d in FAR]
 
-    def second_copies(src, G2, s, q):
-        return [rc(src, G2.at[sx], s.at[d - 1], q.at[d - 1], {"sx": lax.rem(sx + d, SIDE)}) for d in FAR]
-
     a1 = first_copies(G1a, a1_s, a1_r)
-    a2 = second_copies(G1a, G2a, a2_s, a2_r)
-    b1 = first_copies(G1b, b1_s, b1_r)
-    b2 = second_copies(G2b.at[sx], G2b, b2_s, b2_r)
-    d1 = first_copies(G1d, d1_s, d1_r)
-    d2 = second_copies(G2d.at[sx], G2d, d2_s, d2_r)
     mine_y, mine_x = pl.ds(sy, 1), pl.ds(sx, 1)
 
-    def half_sum(G1, G2, one, two):
-        each(one, "wait")
-        G2[mine_x] = jnp.sum(G1[...], axis=0, keepdims=True)
-        each(two, "start")
-
-    def full_sum(G2, two):
-        each(two, "wait")
-        return jnp.sum(G2[...], axis=0)
-
-    G1b[mine_y] = jnp.broadcast_to(cnt_ref[...], (1, 2, SUB, LANES))
-    each(b1, "start")
+    def gather(G, s, q):
+        me = SIDE * sx + sy
+        return me, [rc(G.at[me], G.at[me], s.at[k], q.at[k], peer) for k, peer in enumerate(peers)]
+    sub4 = lax.broadcasted_iota(jnp.int32, (SIDE, LANES), 0)
+
+    def send_rows(G, s, q, rows):
+        me, copies = gather(G, s, q)
+        v = jnp.zeros((SIDE, LANES), F32)
+        for k, one in enumerate(rows):
+            v = jnp.where(sub4 == k, one, v)
+        G[pl.ds(me, 1)] = v[None]
+        each(copies, "start")
+
+    def full_sum(G, s, q):
+        each(gather(G, s, q)[1], "wait")
+        return jnp.sum(G[...], axis=0)
+
+    send_rows(Gb, b_s, b_r, [row(cnt_ref[...], 0)])
 
     def halos(slabs, hs, hr, vs, vr):
         h = [rc(S48.at[slabs, own, pl.ds(SUB, SUB)], S48.at[slabs, own, pl.ds(ME, SUB)], hs.at[0], hr.at[0], left),
@@ -222,7 +221,6 @@
 
     for at in (0, LAST * CHUNK + BT):
         put_l(restrict, pl.ds(at, BT))
-    half_sum(G1b, G2b, b1, b2)
 
     def split_inv(c):
         inv_cp[c].wait()
@@ -250,7 +248,7 @@
             total = total + dot(lhs(LANES * (n // 2)), jnp.concatenate(two, axis=0))
         return total
 
-    cnt = full_sum(G2b, b2)[0]
+    cnt = wide(row(full_sum(Gb, b_s, b_r), 0))
     lane = lax.broadcasted_iota(jnp.int32, (SUB, LANES), 1)
     starts = cnt
     for d in (KMAX, 2 * KMAX, D * KMAX, SUB * KMAX):
@@ -381,8 +379,12 @@
                     T[h, pl.ds(top, whole), off:off + n // whole] = v[0:n, lanes(h)].reshape(whole, n // whole, LANES)
                 v, at = v[n:], at + n
 
-    def v_copy(e):
-        return rc(T.at[:, pl.ds(1 + (M - 1) * e, STRIP)], V.at[1 - e], v_s.at[e], v_r.at[1 - e], {"sx": sx - 1 + 2 * e})
+    def v_copy(e, par):
+        return rc(T.at[:, pl.ds(1 + (M - 1) * e, STRIP)], V.at[par, 1 - e], v_s.at[e], v_r.at[par, 1 - e], {"sx": sx - 1 + 2 * e})
+
+    def v_wait(e, par):
+        v_copy(e, par).wait_send()
+        rc(T.at[:, pl.ds(1, STRIP)], V.at[par, e], v_s.at[e], v_r.at[par, e], left).wait_recv()
 
     def step(m, carry):
         par = lax.rem(m, 2)
@@ -395,38 +397,53 @@
 
         mids = [side(n, cols(T, EDGE + ROWS * n, ROWS), HB.at[:, :, n]) for n in HALVES]
         edges = [side(2 + e, cols(TE, EDGE * e, EDGE), HE.at[:, :, e]) for e in (near, 1 - near)]
-        ring = side(SIDE, (PK.at[0], PK.at[1]), HP)
-        everything = mids + edges + [ring]
-        v_near, v_far = v_copy(near), v_copy(1 - near)
+        rings = [side(SIDE + n, [PK.at[j, :, pl.ds(at, size)] for j in HALVES], HP.at[:, :, :, pl.ds(at, size)])
+                 for n, (at, size) in enumerate(((mult(BT * (1 - near)), ME - BT), (mult((ME - BT) * near, SUB), BT)))]
+        everything = mids + edges + rings
+        v_near, v_far = v_copy(near, par), v_copy(1 - near, par)
+        a2 = [rc(G1a, G2a.at[par, sx], a2_s.at[d - 1], a2_r.at[par, d - 1], {"sx": lax.rem(sx + d, SIDE)}) for d in FAR]
 
         def edge(e, pair):
             for h in HALVES:
-                TE[h, pl.ds((EDGE + 2) * e, STRIP)] = T[h, pl.ds((M + 1) * e, STRIP)] + V[e, h]
+                TE[h, pl.ds((EDGE + 2) * e, STRIP)] = T[h, pl.ds((M + 1) * e, STRIP)] + V[par, e, h]
                 TE[h, pl.ds(STRIP + 2 * e, 2)] = T[h, pl.ds(STRIP + 2 * EDGE * e, 2)]
             go(pair)
 
+        def ring_rows(pairs):
+            for h in HALVES:
+                for at, ref, k in pairs:
+                    for j, lane in enumerate((SUB, M - 1)):
+                        PK[j, h, at] = ref[h, k, lane:lane + 1]
+
+        def ring_edge(e):
+            for h in HALVES:
+                for k in range(ROWS):
+                    for j, lane in enumerate((SUB, M - 1)):
+                        PK[j, h, pl.ds((M - 2) * e + k, 1)] = TE[h, pl.ds(ROWS * e + 1 + k, 1), lane:lane + 1].reshape(1, LANES)
+
         first = m == 0
-        c0, c3 = LAST * near, LAST * (1 - near)
-        for h in HALVES:
-            G1d[mine_y, h] = pqs[h][None]
-        each(d1, "start")
-        out = product((LAST * CHUNK + BT) * near, CHUNK + BT)
-        put_t([out[0][BT:], out[1]], c0)
+        c_near, c_far = LAST * near, LAST * (1 - near)
+        start = (LAST * CHUNK + BT) * near
+        send_rows(Gd, d_s, d_r, [row(pqs[h], 0) for h in HALVES])
+        out = product((LAST * CHUNK + BT) - start, CHUNK + BT)
+        put_t([out[0][BT:], out[1]], c_far)
         for h in HALVES:
             G1a[mine_y, h] = out[0][0:SUB, lanes(h)][None]
         each(a1, "start")
+        v_far.start()
+        put_t(product(BT + start, CHUNK), c_near)
         pl.when(inner)(v_near.start)
         pl.when(jnp.logical_not(inner))(lambda: edge(near, edges[0]))
+        v_wait(1 - near, par)
+        edge(1 - near, edges[1])
         put_t(product(BT + CHUNK, CHUNK), 1)
         go(mids[0])
-        half_sum(G1d, G2d, d1, d2)
-        put_t(product(BT + 2 * CHUNK, CHUNK), 2)
-        go(mids[1])
         each(a1, "wait")
         each(a2, "start")
 
-        pq = full_sum(G2d, d2)
-        alpha = [jnp.where(first, -1.0, row(cst[0, h], 0) / row(pq[h], 0)) for h in HALVES]
+        pq = full_sum(Gd, d_s, d_r)
+        alpha = [jnp.where(first, -1.0, row(cst[0, h], 0) / row(pq, h)) for h in HALVES]
+
         tot = [[zero, zero] for h in HALVES]
 
         def update(c, inside):
@@ -442,38 +459,30 @@
                     tot[h][0] = tot[h][0] + rn * ln
                     tot[h][1] = tot[h][1] + w * (rn * rn)
 
-        out = product(BT + (LAST * CHUNK + BT) * (1 - near), CHUNK)
-        update(c0, False)
+        out = product(BT + 2 * CHUNK, CHUNK)
+        update(c_far, False)
+        update(c_near, False)
         update(1, True)
+        put_t(out, 2)
+        go(mids[1])
         update(2, True)
-        put_t(out, c3)
-        v_far.start()
-        G2a[mine_x] = G1a[...][None]
+        G2a[par, mine_x] = G1a[...][None]
         each(a2, "wait_send")
-        update(c3, False)
-        for h in HALVES:
-            G1b[mine_y, h] = jnp.where(sub8 == 0, colsum(tot[h][0]), jnp.where(sub8 == 1, colsum(tot[h][1]), 0.0))[None]
-        each(b1, "start")
+        send_rows(Gb, b_s, b_r, [colsum(v) for two in tot for v in two])
+        ring_rows([(slice(i - 1, i), T, i) for i in range(EDGE, M - 1)])
+        ring_edge(1 - near)
+        go(rings[0])
 
         @pl.when(inner)
         def _():
-            v_near.wait_send()
-            rc(T.at[:, pl.ds(1, STRIP)], V.at[near], v_s.at[near], v_r.at[near], left).wait_recv()
+            v_wait(near, par)
             edge(near, edges[0])
-
-        v_far.wait_send()
-        rc(T.at[:, pl.ds(1, STRIP)], V.at[1 - near], v_s.at[near], v_r.at[1 - near], left).wait_recv()
-        edge(1 - near, edges[1])
-        for h in HALVES:
-            for i in range(1, ME + 1):
-                src, k = (TE, i) if i < EDGE else ((T, i) if i < M - 1 else (TE, i - 2 * ROWS))
-                PK[0, h, i - 1:i] = src[h, k, SUB:SUB + 1]
-                PK[1, h, i - 1:i] = src[h, k, M - 1:M]
-        go(ring)
+        ring_edge(near)
+        go(rings[1])
 
         pl.when(first)(geometry)
         each(a2, "wait_recv")
-        cq = jnp.concatenate([G2a[:, :, h].reshape(LANES, LANES) for h in HALVES], axis=1)
+        cq = jnp.concatenate([G2a[par, :, :, h].reshape(LANES, LANES) for h in HALVES], axis=1)
         yq = dot_pieces(lambda at: Ccat[:, at:at + TILE], cq)
         rzc = []
         for h in HALVES:
@@ -486,12 +495,11 @@
             for h in HALVES:
                 Ey[h, n * part:n * (part + 1)] = o[:, lanes(h)].reshape(n, ME, LANES)
 
-        half_sum(G1b, G2b, b1, b2)
-        got = full_sum(G2b, b2)
+        got = full_sum(Gb, b_s, b_r)
         beta = []
         for h in HALVES:
-            rzn = row(got[h], 0) + rzc[h]
-            rr = row(got[h], 1)
+            rzn = row(got, 2 * h) + rzc[h]
+            rr = row(got, 2 * h + 1)
             beta.append(jnp.where(first, 0.0, rzn / row(cst[0, h], 0)))
             ff = jnp.where(first, jnp.sqrt(rr), row(cst[1, h], 0))
             cst[0, h] = wide(rzn)
@@ -558,12 +566,9 @@
 
     lax.fori_loop(0, ITERS, step, 0)
 
-    for h in HALVES:
-        G1d[mine_y, h] = pqs[h][None]
-    each(d1, "start")
-    half_sum(G1d, G2d, d1, d2)
-    pq = full_sum(G2d, d2)
-    alpha = [row(cst[0, h], 0) / row(pq[h], 0) for h in HALVES]
+    send_rows(Gd, d_s, d_r, [row(pqs[h], 0) for h in HALVES])
+    pq = full_sum(Gd, d_s, d_r)
+    alpha = [row(cst[0, h], 0) / row(pq, h) for h in HALVES]
 
     def finish(i, car):
         res = []
@@ -576,13 +581,10 @@
     rr = lax.fori_loop(OWN, OWN + M, finish, (zero, zero))
     out_cp = [pltpu.make_async_copy(T.at[h, own, pl.ds(0, M)], x_hbm.at[:, :, pl.ds(LANES * h, LANES)], out_sem.at[h]) for h in HALVES]
     each(out_cp, "start")
+    send_rows(Gb, b_s, b_r, [colsum(v) for v in rr])
+    got = full_sum(Gb, b_s, b_r)
     for h in HALVES:
-        G1b[mine_y, h] = wide(colsum(rr[h]))[None]
-    each(b1, "start")
-    half_sum(G1b, G2b, b1, b2)
-    got = full_sum(G2b, b2)
-    for h in HALVES:
-        nrm_ref[:, lanes(h)] = jnp.where(sub8 == ITERS - 1, jnp.sqrt(row(got[h], 0)) / row(cst[1, h], 0), nrm_ref[:, lanes(h)])
+        nrm_ref[:, lanes(h)] = jnp.where(sub8 == ITERS - 1, jnp.sqrt(row(got, h)) / row(cst[1, h], 0), nrm_ref[:, lanes(h)])
     each(out_cp, "wait")
 
 
@@ -595,15 +597,16 @@
 
     field = vm(2, LOW, ME, LANES)
     strips = [vm(2, 2, 2, 2, n, SUB, LANES) for n in (ROWS, EDGE)]
-    gathers = [vm(SIDE, 2, SUB, LANES), vm(SIDE, SIDE, 2, SUB, LANES)] + [vm(SIDE, 2, SUB, LANES)] * SIDE
+    gathers = [vm(SIDE, 2, SUB, LANES), vm(2, SIDE, SIDE, 2, SUB, LANES)] + [vm(SIDE * SIDE, SIDE, LANES)] * 2
     scratch = [
         vm(len(PIECES), M + 2 * OWN, WIDE, LANES), vm(NL, KM * len(PIECES), dtype=BF16), vm(NL, 2 * TILE, dtype=BF16),
         vm(SIDE, CHUNK, NE), vm(len(PIECES), KM, TILE, dtype=BF16), vm(2 * TILE, TILE, dtype=BF16),
         field, vm(2, 2 * EDGE, ME, LANES), field, field, field, field, field, field, field,
         vm(SIDE + 1, ME, ME, LANES), vm(LOW * ME, LANES * len(PIECES), dtype=BF16), vm(2, ME, LANES), vm(M + 2 * OWN, WIDE, LANES), vm(LANES, NP),
-        vm(2, 2, STRIP, ME, LANES), *strips, vm(2, 2, 2, ME, LANES), vm(2, 2, ME, LANES), *gathers,
+        vm(2, 2, 2, STRIP, ME, LANES), *strips, vm(2, 2, 2, ME, LANES), vm(2, 2, ME, LANES), *gathers,
         vm(LANES, LANES * len(PIECES), dtype=BF16), vm(2, LANES, LANES), vm(2, LANES, LANES), vm(2, 2, SUB, LANES),
-        vm(2, SUB, LANES), dma(SIDE), dma(2), *[dma(2)] * 10, *[dma(2, 2, SIDE + 1)] * 2, *[dma(LAST)] * 12, dma(2),
+        vm(2, SUB, LANES), dma(SIDE), dma(2), *[dma(2)] * 9, dma(2, 2), *[dma(2, 2, SIDE + 2)] * 2,
+        *[dma(LAST)] * 3, dma(2, LAST), *[dma(SIDE * SIDE - 1)] * 4, dma(2),
     ]
     any_spec = pl.BlockSpec(memory_space=pl.ANY)
     vmem_spec = pl.BlockSpec(memory_space=pltpu.VMEM)

time: 213 us -> 186 us (0.87)
  Pallas kernels: 205 us -> 178 us
    pallas_call x1, Pallas kernels: 205 us -> 178 us  [body(): pl.pallas_call(solve_kernel, out_shape=(jax.ShapeDtypeStruct((M, M, 2 * L...]
where the time goes in v4:
time: 186 us
  Pallas kernels  178 us (96%)
  local copies, waits for them, and re-layouts  4.99 us (3%)
    pallas_call x1, Pallas kernels, body(): pl.pallas_call(solve_kernel, out_shape=(jax.ShapeDtypeStruct((M, M, 2 * L...  178 us

profile of v4, /device:TPU:0, one launch (start us, length us, event | category | flops | bytes accessed | tf_op | source)
XLA Modules:
  0.0 186.0 jit_solution(13596001645317906276)
XLA Ops:
  1.3 0.6 broadcast_in_dim.23.cnt_ref
  1.9 0.8 reshape.22
  2.7 1.4 pad_maximum_fusion.own_ref
  4.1 178.3 %shard_map.77 = (f32[32,32,256]{2,1,0:T(8,128)}, f32[8,256]{1,0:T(8,128)}) custom-call(f32[32,32,256]{2,1,0:T(8,128)} %f_hbm.1, f32[1600,1600]{1,0:T(8,128)} %bitcast.6, f32[8,1024]{1,0:T(8,128)} %pad_maximum_fusion.own_ref, f32[64,64]{1,0:T(8,128)} %cinv_ref.1, f32[8,128]{1,0:T(8,128)} %broadcast_in_dim.23.cnt_ref), custom_call_target="tpu_custom_call" | custom-call | tf_op jit(solution)/shard_map/pallas_call | solution.py:619
  182.4 2.3 %copy.11 = f32[32,32,256]{2,1,0:T(8,128)} copy(f32[32,32,256]{2,1,0:T(8,128)} %get-tuple-element.4) | data formatting | bytes 2097152
  184.7 1.3 copy.12
  (1 shorter events, 0.0 us)

commit v5 on v4

--- a/solution.py
+++ b/solution.py
@@ -331,16 +331,12 @@
 
     def put_x(two, h, k):
         v, rows = pair_of(two, k)
-        pieces = split3(v)
-        if isinstance(k, int) and k == ME // 2 - 1:
-            n = KM - 2 * ME * k
-            for j, piece in enumerate(pieces):
-                X[j, KM - n:KM, lanes(h)] = piece[0:n]
-            for slot, j in enumerate((0, 0, 1, 1, 2, 0)):
-                Xr[REM * slot:REM * (slot + 1), lanes(h)] = pieces[j][n:]
-        else:
-            for j, piece in enumerate(pieces):
-                X[j, rows, lanes(h)] = piece
+        for j, piece in enumerate(split3(v)):
+            X[j, rows, lanes(h)] = piece
+
+    def put_rest():
+        for slot, j in enumerate((0, 0, 1, 1, 2, 0)):
+            Xr[REM * slot:REM * (slot + 1), :] = X[j, KM:NE, :]
 
     def first_rows(k, c):
         for h in HALVES:
@@ -349,8 +345,8 @@
                 Q[h, 2 * k + 1 + j] = two[j]
             put_x(two, h, k)
         return c
-    lax.fori_loop(0, ME // 2 - 1, first_rows, 0)
-    first_rows(ME // 2 - 1, 0)
+    lax.fori_loop(0, ME // 2, first_rows, 0)
+    put_rest()
 
     colf = jnp.where((jcol >= D) & (jcol < D + M), 1.0, 0.0)
     sub8 = lax.broadcasted_iota(jnp.int32, (SUB, LANES), 0)
@@ -364,7 +360,7 @@
             total = dot(Lr[rows, :], Xr[...])
             for j in PIECES:
                 for i in PIECES[:len(PIECES) - j]:
-                    total = total + dot(L[rows, KM * i:KM * (i + 1)], X[j])
+                    total = total + dot(L[rows, KM * i:KM * (i + 1)], X[j, 0:KM, :])
             outs.append(total)
         return outs
 
@@ -397,8 +393,9 @@
 
         mids = [side(n, cols(T, EDGE + ROWS * n, ROWS), HB.at[:, :, n]) for n in HALVES]
         edges = [side(2 + e, cols(TE, EDGE * e, EDGE), HE.at[:, :, e]) for e in (near, 1 - near)]
+        parts = ((mult(BT * (1 - near)), ME - BT), (mult((ME - BT) * near, SUB), BT))
         rings = [side(SIDE + n, [PK.at[j, :, pl.ds(at, size)] for j in HALVES], HP.at[:, :, :, pl.ds(at, size)])
-                 for n, (at, size) in enumerate(((mult(BT * (1 - near)), ME - BT), (mult((ME - BT) * near, SUB), BT)))]
+                 for n, (at, size) in enumerate(parts)]
         everything = mids + edges + rings
         v_near, v_far = v_copy(near, par), v_copy(1 - near, par)
         a2 = [rc(G1a, G2a.at[par, sx], a2_s.at[d - 1], a2_r.at[par, d - 1], {"sx": lax.rem(sx + d, SIDE)}) for d in FAR]
@@ -464,11 +461,11 @@
         update(c_near, False)
         update(1, True)
         put_t(out, 2)
-        go(mids[1])
         update(2, True)
         G2a[par, mine_x] = G1a[...][None]
         each(a2, "wait_send")
         send_rows(Gb, b_s, b_r, [colsum(v) for two in tot for v in two])
+        go(mids[1])
         ring_rows([(slice(i - 1, i), T, i) for i in range(EDGE, M - 1)])
         ring_edge(1 - near)
         go(rings[0])
@@ -506,9 +503,6 @@
             cst[1, h] = wide(ff)
             nrm_ref[:, lanes(h)] = jnp.where(sub8 == m - 1, jnp.sqrt(rr) / ff, nrm_ref[:, lanes(h)])
 
-        for pair in everything:
-            come(pair)
-
         def renew(i, u):
             for h in HALVES:
                 zn = z[h, i] - alpha[h] * (u[h] + Ey[h, i])
@@ -518,20 +512,30 @@
         def sides(b, buf, n, h, k):
             return jnp.concatenate([b[0:SUB] + buf[par, 0, n, h, k], b[SUB:M], b[M:] + buf[par, 1, n, h, k]], axis=0)
 
-        def mid_rows(k, c):
-            for n in HALVES:
+        def mid_rows(n):
+            def body(k, c):
                 i = EDGE + ROWS * n + k
                 renew(i, [sides(T[h, i], HB, n, h, k) for h in HALVES])
-            return c
-        lax.fori_loop(0, ROWS, mid_rows, 0)
-
-        def edge_rows(k, c):
-            for n in HALVES:
-                renew((M - 1) * n + k, [sides(TE[h, EDGE * n + k], HE, n, h, k) for h in HALVES])
-            return c
-        lax.fori_loop(0, EDGE, edge_rows, 0)
-        for j in HALVES:
-            renew(LOW - 2 + j, [HP[par, j, h] for h in HALVES])
+                return c
+            come(mids[n])
+            lax.fori_loop(0, ROWS, body, 0)
+
+        def edge_rows(e, pair):
+            def body(k, c):
+                renew((M - 1) * e + k, [sides(TE[h, EDGE * e + k], HE, e, h, k) for h in HALVES])
+                return c
+            come(pair)
+            lax.fori_loop(0, EDGE, body, 0)
+
+        def ring_cells(n):
+            come(rings[n])
+            at = pl.ds(*parts[n])
+            for h in HALVES:
+                for j in HALVES:
+                    i = LOW - 2 + j
+                    zn = z[h, i, at] - alpha[h] * (HP[par, j, h, at] + Ey[h, i, at])
+                    z[h, i, at] = zn
+                    p[h, i, at] = zn + beta[h] * p[h, i, at]
 
         def apply_rows(g, car):
             sums = list(car)
@@ -555,8 +559,17 @@
                         put_x(rows[h], h, D * g + k // 2)
                         rows[h] = []
             return tuple(sums)
-        car = lax.fori_loop(0, ME // SUB - 1, apply_rows, (zero, zero))
-        car = apply_rows(ME // SUB - 1, car)
+        edge_rows(1 - near, edges[1])
+        mid_rows(0)
+        mid_rows(1)
+        ring_cells(0)
+        low = 2 * (1 - near)
+        car = lax.fori_loop(low, low + LAST, apply_rows, (zero, zero))
+        edge_rows(near, edges[0])
+        ring_cells(1)
+        low = LAST * near
+        car = lax.fori_loop(low, low + 2, apply_rows, car)
+        put_rest()
         for h in HALVES:
             pqs[h] = wide(colsum(car[h]))
 
@@ -600,7 +613,7 @@
     gathers = [vm(SIDE, 2, SUB, LANES), vm(2, SIDE, SIDE, 2, SUB, LANES)] + [vm(SIDE * SIDE, SIDE, LANES)] * 2
     scratch = [
         vm(len(PIECES), M + 2 * OWN, WIDE, LANES), vm(NL, KM * len(PIECES), dtype=BF16), vm(NL, 2 * TILE, dtype=BF16),
-        vm(SIDE, CHUNK, NE), vm(len(PIECES), KM, TILE, dtype=BF16), vm(2 * TILE, TILE, dtype=BF16),
+        vm(SIDE, CHUNK, NE), vm(len(PIECES), NE, TILE, dtype=BF16), vm(2 * TILE, TILE, dtype=BF16),
         field, vm(2, 2 * EDGE, ME, LANES), field, field, field, field, field, field, field,
         vm(SIDE + 1, ME, ME, LANES), vm(LOW * ME, LANES * len(PIECES), dtype=BF16), vm(2, ME, LANES), vm(M + 2 * OWN, WIDE, LANES), vm(LANES, NP),
         vm(2, 2, 2, STRIP, ME, LANES), *strips, vm(2, 2, 2, ME, LANES), vm(2, 2, ME, LANES), *gathers,

time: 186 us -> 182 us (0.978)
  Pallas kernels: 178 us -> 174 us
    pallas_call x1, Pallas kernels: 178 us -> 174 us  [body(): pl.pallas_call(solve_kernel, out_shape=(jax.ShapeDtypeStruct((M, M, 2 * L...]
where the time goes in v5:
time: 182 us
  Pallas kernels  174 us (96%)
  local copies, waits for them, and re-layouts  4.99 us (3%)
    pallas_call x1, Pallas kernels, body(): pl.pallas_call(solve_kernel, out_shape=(jax.ShapeDtypeStruct((M, M, 2 * L...  174 us

profile of v5, /device:TPU:0, one launch (start us, length us, event | category | flops | bytes accessed | tf_op | source)
XLA Modules:
  0.0 182.1 jit_solution(7493638739749504125)
XLA Ops:
  1.3 0.6 broadcast_in_dim.23.cnt_ref
  1.9 0.8 reshape.22
  2.7 1.4 pad_maximum_fusion.own_ref
  4.1 174.4 %shard_map.77 = (f32[32,32,256]{2,1,0:T(8,128)}, f32[8,256]{1,0:T(8,128)}) custom-call(f32[32,32,256]{2,1,0:T(8,128)} %f_hbm.1, f32[1600,1600]{1,0:T(8,128)} %bitcast.6, f32[8,1024]{1,0:T(8,128)} %pad_maximum_fusion.own_ref, f32[64,64]{1,0:T(8,128)} %cinv_ref.1, f32[8,128]{1,0:T(8,128)} %broadcast_in_dim.23.cnt_ref), custom_call_target="tpu_custom_call" | custom-call | tf_op jit(solution)/shard_map/pallas_call | solution.py:632
  178.5 2.3 %copy.11 = f32[32,32,256]{2,1,0:T(8,128)} copy(f32[32,32,256]{2,1,0:T(8,128)} %get-tuple-element.4) | data formatting | bytes 2097152
  180.8 1.3 copy.12
  (1 shorter events, 0.0 us)

commit v6 on v5

--- a/solution.py
+++ b/solution.py
@@ -78,7 +78,7 @@
 
 
 def solve_kernel(f_hbm, inv_hbm, own_ref, cinv_ref, cnt_ref, x_hbm, nrm_ref,
-                 S48, L, Lr, stage, X, Xr, T, TE, z, p, r, l, x, Q, Ey, W5, Ecat, RE, KB, FL,
+                 S48, L, Lr, stage, X, Xr, T, TE, z, p, r, l, x, Q, Ey, W5, Ecat, RE, KB, FL, PF, RF,
                V, HB, HE, HP, PK, G1a, G2a, Gb, Gd, Ccat, cr, wr, cst, pqs,
                ld_sem, own_sem, h0_s, h0_r, v0_s, v0_r, h1_s, h1_r, v1_s, v1_r, v_s, v_r, hm_s, hm_r,
                a1_s, a1_r, a2_s, a2_r, b_s, b_r, d_s, d_r, out_sem):
@@ -104,7 +104,7 @@
     zcol = jnp.zeros((len(PIECES), M, SUB, LANES), F32)
     S48[:, OWN:OWN + M, 0:SUB] = zcol
     S48[:, OWN:OWN + M, ME:] = zcol
-    for b in (V, HB, HE, HP):
+    for b in (V, HB, HE, HP, RF):
         b[...] = jnp.zeros(b.shape, F32)
 
     bar = pltpu.get_barrier_semaphore()
@@ -145,7 +145,8 @@
              rc(S48.at[slabs, pl.ds(M, OWN)], S48.at[slabs, pl.ds(0, OWN)], vs.at[1], vr.at[0], {"sx": sx + 1})]
         v_in = [rc(S48.at[slabs, pl.ds(0, OWN)], S48.at[slabs, pl.ds(0, OWN)], vs.at[e], vr.at[e], left) for e in HALVES]
         return h, v, v_in
-    f_h, f_v, f_in = halos(pl.ds(0, 2), h0_s, h0_r, v0_s, v0_r)
+    _, f_v, f_in = halos(pl.ds(0, 2), h0_s, h0_r, v0_s, v0_r)
+    f_h = [rc(PF.at[j], RF.at[1 - j], h0_s.at[j], h0_r.at[j], (left, right)[j]) for j in HALVES]
     k_h, k_v, k_in = halos(pl.ds(2, 1), h1_s, h1_r, v1_s, v1_r)
 
     def go(pair):
@@ -164,6 +165,24 @@
         for e in HALVES:
             pl.when(has[e])(getattr(pair[e], what))
     each(own_cp, "wait")
+    lower = lax.broadcasted_iota(jnp.int32, (SUB, LANES), 0) < D
+
+    def pack(k, c):
+        for h in HALVES:
+            for j in HALVES:
+                a, b = [S48[h, OWN + 2 * k + n, (M if j else SUB):(ME if j else 2 * SUB)] for n in HALVES]
+                PF[j, h, k] = jnp.where(lower, pltpu.roll(a, D, 0), b) if j else jnp.where(lower, a, pltpu.roll(b, D, 0))
+        return c
+
+    def unpack(k, c):
+        for h in HALVES:
+            for j in HALVES:
+                v = RF[j, h, k]
+                two = (v, pltpu.roll(v, D, 0))
+                for n in HALVES:
+                    S48[h, OWN + 2 * k + n, (ME if j else 0):(WIDE if j else SUB)] = two[n if j else 1 - n]
+        return c
+    lax.fori_loop(0, M // 2, pack, 0)
     go(f_h)
 
     slot = mult(KMAX * (sx * SIDE + sy), KMAX)
@@ -234,6 +253,7 @@
     split_inv(1)
     come(f_h)
     gone(f_h)
+    lax.fori_loop(0, M // 2, unpack, 0)
     up_down(f_v, "start")
     split_inv(2)
     split_inv(LAST)
@@ -616,6 +636,7 @@
         vm(SIDE, CHUNK, NE), vm(len(PIECES), NE, TILE, dtype=BF16), vm(2 * TILE, TILE, dtype=BF16),
         field, vm(2, 2 * EDGE, ME, LANES), field, field, field, field, field, field, field,
         vm(SIDE + 1, ME, ME, LANES), vm(LOW * ME, LANES * len(PIECES), dtype=BF16), vm(2, ME, LANES), vm(M + 2 * OWN, WIDE, LANES), vm(LANES, NP),
+        *[vm(2, 2, M // 2, SUB, LANES)] * 2,
         vm(2, 2, 2, STRIP, ME, LANES), *strips, vm(2, 2, 2, ME, LANES), vm(2, 2, ME, LANES), *gathers,
         vm(LANES, LANES * len(PIECES), dtype=BF16), vm(2, LANES, LANES), vm(2, LANES, LANES), vm(2, 2, SUB, LANES),
         vm(2, SUB, LANES), dma(SIDE), dma(2), *[dma(2)] * 9, dma(2, 2), *[dma(2, 2, SIDE + 2)] * 2,

time: 182 us -> 181 us (level)
  no operation moved by 1% of the time
where the time goes in v6:
time: 181 us
  Pallas kernels  173 us (96%)
  local copies, waits for them, and re-layouts  4.99 us (3%)
    pallas_call x1, Pallas kernels, body(): pl.pallas_call(solve_kernel, out_shape=(jax.ShapeDtypeStruct((M, M, 2 * L...  173 us

profile of v6, /device:TPU:0, one launch (start us, length us, event | category | flops | bytes accessed | tf_op | source)
XLA Modules:
  0.0 180.9 jit_solution(9936994258319921225)
XLA Ops:
  1.3 0.6 broadcast_in_dim.23.cnt_ref
  1.9 0.8 reshape.22
  2.7 1.4 pad_maximum_fusion.own_ref
  4.1 173.2 %shard_map.77 = (f32[32,32,256]{2,1,0:T(8,128)}, f32[8,256]{1,0:T(8,128)}) custom-call(f32[32,32,256]{2,1,0:T(8,128)} %f_hbm.1, f32[1600,1600]{1,0:T(8,128)} %bitcast.6, f32[8,1024]{1,0:T(8,128)} %pad_maximum_fusion.own_ref, f32[64,64]{1,0:T(8,128)} %cinv_ref.1, f32[8,128]{1,0:T(8,128)} %broadcast_in_dim.23.cnt_ref), custom_call_target="tpu_custom_call" | custom-call | tf_op jit(solution)/shard_map/pallas_call | solution.py:653
  177.3 2.3 %copy.11 = f32[32,32,256]{2,1,0:T(8,128)} copy(f32[32,32,256]{2,1,0:T(8,128)} %get-tuple-element.4) | data formatting | bytes 2097152
  179.6 1.3 copy.12
  (1 shorter events, 0.0 us)
